TPU v7x, 128 devices: a whole 4x4x4 slice. The times are simulated.
128 devices in a mesh: ox: 8 (over z, x_lo), oy: 16 (over x_hi, y, core).
Axes of the slice: x: 4 (x_hi: 2, x_lo: 2; x = x_hi * 2 + x_lo), y: 4, z: 4, core: 2. Of those that a mesh axis runs over, the one named last changes fastest.
Arguments:
- zonal_flow: float32 [4, 1024, 2048], P(None, 'ox', 'oy'), may hold values from -3 to 3
- merid_flow: float32 [4, 1024, 2048], P(None, 'ox', 'oy'), may hold values from -3 to 3
- thickness: float32 [4, 1024, 2048], P(None, 'ox', 'oy'), may hold values from 0.8 to 2
- land_sea: int32 [1024, 2048], P('ox', 'oy'), may hold values 0 or 1
- viscosity: float32 [1024, 2048], P('ox', 'oy'), may hold values from 0.2 to 3
- wind_stress: float32 [2, 1024, 2048], P(None, 'ox', 'oy'), may hold values from -5 to 5
- reduced_gravity: float32 [4], replicated, may hold values from 0.1 to 1
- conv_first: bfloat16 [3, 3, 64, 4], replicated, may hold values from -1 to 1
- bias_first: float32 [64], replicated, may hold values from -3 to 3
- conv_second: bfloat16 [3, 3, 64, 64], replicated, may hold values from -0.25 to 0.25
- bias_second: float32 [64], replicated, may hold values from -3 to 3
- conv_last: bfloat16 [3, 3, 1, 64], replicated, may hold values from -0.25 to 0.25
Outputs:
- zonal_next: float32 [4, 1024, 2048], P(None, 'ox', 'oy')
- merid_next: float32 [4, 1024, 2048], P(None, 'ox', 'oy')
- thickness_next: float32 [4, 1024, 2048], P(None, 'ox', 'oy')
- viscosity_next: float32 [1024, 2048], P('ox', 'oy')
Inputs may be any that keep to these rules, and one draw needn't show every extreme that they name: `land_sea`: 1 marks a sea cell.
All inputs are finite; a program needn't handle non-finite values. No bound on the sum of `land_sea` on one device may be relied on, other than what follows from the above.
Results may differ from a plain program's by a relative error of at most 0.0019.
Values may be sent and summed in bfloat16 or wider, within the bound.
A program may use at most 192 MiB of HBM per device.

v0:
```python
import jax
import jax.numpy as jnp
from jax import lax
from jax.sharding import Mesh
from jax.sharding import PartitionSpec as P

OY = ("oy_0", "oy_1", "oy_2")
OX_OY = ("ox", "oy_0", "oy_1", "oy_2")


TIME_STEP = 0.05
REST_DEPTH = 1.4
DRAG_RATE = 0.5


def with_halo(block, sides, width, periodic):
    for axis, dim in sides:
        count = lax.axis_size(axis)
        forward = [(i, i + 1) for i in range(count - 1)]
        if periodic:
            forward.append((count - 1, 0))
        backward = [(target, source) for source, target in forward]
        low = lax.ppermute(
            lax.slice_in_dim(block, block.shape[dim] - width, None, axis=dim), axis, forward
        )
        high = lax.ppermute(lax.slice_in_dim(block, 0, width, axis=dim), axis, backward)
        block = jnp.concatenate([low, block, high], axis=dim)
    return block


def extended_2(x, sides, width):
    edges = {}
    for axis, dim in sides:
        size, length = (lax.axis_size(axis), x.shape[dim])
        up = [(i, (i + 1) % size) for i in range(size)]
        last = lax.slice_in_dim(x, length - width, length, axis=dim)
        first = lax.slice_in_dim(x, 0, width, axis=dim)
        edges[dim] = (
            lax.ppermute(last, axis, up),
            lax.ppermute(first, axis, [(b, a) for a, b in up]),
        )
    done = []
    for _, dim in sides:
        low, high = edges[dim]
        around = [(width, width) if d in done else (0, 0) for d in range(x.ndim)]
        x = jnp.concatenate([jnp.pad(low, around), x, jnp.pad(high, around)], axis=dim)
        done.append(dim)
    return x


def in_blocks(x, dim, size):
    dims = x.shape
    pieces = x.reshape(*dims[:dim], size, dims[dim] // size, *dims[dim + 1 :])
    return jnp.moveaxis(pieces, dim, 0)


def in_order(pieces, dim):
    pieces = jnp.moveaxis(pieces, 0, dim)
    dims = pieces.shape
    return pieces.reshape(*dims[:dim], dims[dim] * dims[dim + 1], *dims[dim + 2 :])


def turned_blocks(pieces, axes, order):
    inside = pieces.shape[1:]
    out = pieces.reshape(*(lax.axis_size(a) for a in axes), *inside)
    for k in order:
        out = lax.all_to_all(out, axes[k], k, k, tiled=True)
    return out.reshape(-1, *inside)


def two_step_exchange(x, groups, order, split_dim, concat_dim):
    size = lax.axis_size(groups[0]) * lax.axis_size(groups[1])
    pieces = in_blocks(x, split_dim, size)
    return in_order(turned_blocks(pieces, groups, order), concat_dim)


def viscous(field, near, visc, visc_near):
    total = 0.5 * (visc + visc_near[0]) * (near[0] - field)
    for side in range(1, 4):
        total = total + 0.5 * (visc + visc_near[side]) * (near[side] - field)
    return total


def conv_valid(extended, weight):
    width = extended.shape[1] - 2
    height = extended.shape[2] - 2
    total = jnp.zeros((weight.shape[2], width, height), jnp.float32)
    for row_off in range(3):
        for col_off in range(3):
            total = total + jnp.einsum(
                "oc,cxy->oxy",
                weight[row_off, col_off],
                extended[:, row_off : row_off + width, col_off : col_off + height],
                preferred_element_type=jnp.float32,
            )
    return total


def run_network(features, widen, conv_first, bias_first, conv_second, bias_second, conv_last):
    hidden = features
    for weight, bias_term in ((conv_first, bias_first), (conv_second, bias_second)):
        summed = conv_valid(widen(hidden), weight) + bias_term[:, None, None]
        hidden = jax.nn.silu(summed).astype(jnp.bfloat16)
    return conv_valid(widen(hidden), conv_last)


def local(
    zonal_flow,
    merid_flow,
    thickness,
    land_sea,
    viscosity,
    wind_stress,
    reduced_gravity,
    conv_first,
    bias_first,
    conv_second,
    bias_second,
    conv_last,
):
    layers, columns, rows = zonal_flow.shape
    sea = land_sea.astype(jnp.float32)
    zonal_m = zonal_flow * sea
    merid_m = merid_flow * sea
    flux_x = zonal_m * thickness
    flux_y = merid_m * thickness
    visc_row = viscosity[None]
    lon_side = with_halo(
        jnp.concatenate([flux_x, zonal_m, merid_m, visc_row], axis=0), (("ox", 1),), 1, True
    )
    lat_side = with_halo(
        jnp.concatenate([flux_y, zonal_m, merid_m, visc_row], axis=0), ((OY, 2),), 1, False
    )
    east_all = lon_side[:, 2:, :]
    west_all = lon_side[:, :-2, :]
    north_all = lat_side[:, :, 2:]
    south_all = lat_side[:, :, :-2]
    diverge = (east_all[:layers] - west_all[:layers]) * 0.5 + (
        north_all[:layers] - south_all[:layers]
    ) * 0.5
    thickness_next = thickness - TIME_STEP * sea * diverge
    anomaly = thickness_next - REST_DEPTH
    interface = jnp.cumsum(anomaly[::-1], axis=0)[::-1]
    pressure = jnp.cumsum(reduced_gravity[:, None, None] * interface, axis=0)
    press_lon = with_halo(pressure, (("ox", 1),), 1, True)
    press_lat = with_halo(pressure, ((OY, 2),), 1, False)
    grad_x = (press_lon[:, 2:, :] - press_lon[:, :-2, :]) * 0.5
    grad_y = (press_lat[:, :, 2:] - press_lat[:, :, :-2]) * 0.5
    last = 3 * layers
    visc_near = (east_all[last], west_all[last], north_all[last], south_all[last])
    zonal_near = tuple(
        (side[layers : 2 * layers] for side in (east_all, west_all, north_all, south_all))
    )
    merid_near = tuple(
        (side[2 * layers : last] for side in (east_all, west_all, north_all, south_all))
    )
    zonal_visc = viscous(zonal_m, zonal_near, viscosity, visc_near)
    merid_visc = viscous(merid_m, merid_near, viscosity, visc_near)
    lat_rows = lax.axis_index(OY) * rows + jnp.arange(rows)
    total_rows = rows * lax.axis_size(OY)
    coriolis = 0.3 + 1.4 * (lat_rows.astype(jnp.float32) + 0.5) / total_rows
    layer_ids = jnp.arange(layers)
    top = (layer_ids == 0).astype(jnp.float32)[:, None, None]
    bottom = (layer_ids == layers - 1).astype(jnp.float32)[:, None, None]
    force_x = wind_stress[0] / thickness_next[0]
    force_y = wind_stress[1] / thickness_next[0]
    zonal_next = sea * (
        zonal_m
        + TIME_STEP
        * (coriolis * merid_m - grad_x + zonal_visc + top * force_x - DRAG_RATE * bottom * zonal_m)
    )
    merid_next = sea * (
        merid_m
        + TIME_STEP
        * (-coriolis * zonal_m - grad_y + merid_visc + top * force_y - DRAG_RATE * bottom * merid_m)
    )
    energy = 0.5 * jnp.sum(
        thickness_next * (zonal_next * zonal_next + merid_next * merid_next), axis=0
    )
    energy = energy / jnp.sum(thickness_next, axis=0)
    features = jnp.stack(
        [zonal_next[0], merid_next[0], sea * (thickness_next[0] - REST_DEPTH), sea * energy]
    ).astype(jnp.bfloat16)
    banded = lax.all_to_all(features, OY, split_axis=1, concat_axis=2, tiled=True)

    def widen_band(field):
        extended = extended_2(field, ((OX_OY, 1),), 1)
        return jnp.pad(extended, ((0, 0), (0, 0), (1, 1)))

    output = run_network(
        banded, widen_band, conv_first, bias_first, conv_second, bias_second, conv_last
    )
    output = two_step_exchange(output, (("oy_0", "oy_1"), "oy_2"), (1, 0), 2, 1)
    viscosity_next = jnp.exp(output[0])
    return (zonal_next, merid_next, thickness_next, viscosity_next)


def solution(mesh):
    split = Mesh(mesh.devices.reshape(mesh.shape["ox"], 2, 4, 2), ("ox", "oy_0", "oy_1", "oy_2"))
    in_specs = (
        P(None, "ox", OY),
        P(None, "ox", OY),
        P(None, "ox", OY),
        P("ox", OY),
        P("ox", OY),
        P(None, "ox", OY),
        P(),
        P(),
        P(),
        P(),
        P(),
        P(),
    )
    out_specs = (P(None, "ox", OY), P(None, "ox", OY), P(None, "ox", OY), P("ox", OY))
    return jax.shard_map(local, mesh=split, in_specs=in_specs, out_specs=out_specs, check_vma=False)
```

profile of v0, /device:TPU:98, one launch (start us, length us, event | category | flops | bytes accessed | tf_op | source)
XLA Modules:
  0.0 173.3 jit_solution(21221038004288556)
XLA Ops:
  4.4 3.6 %collective-permute-start.1 = (f32[13,1,128]{2,1,0:T(1,128)S(1)}, f32[13,1,128]{2,1,0:T(1,128)S(1)}, u32[]{:S(2)}, u32[]{:S(2)}) collective-permute-start(f32[13,1,128]{2,1,0:T(1,128)S(1)} %get-tuple-element.31), channel_id=1, source_target_pairs={{0,16},{16,32},{32,48},{48,64},{64,80},{80,96},{96,112},{112,0},{1... | collective-permute-start | bytes 19976 | tf_op jit(solution)/shard_map/ppermute | solution.py:23
  20.7 4.1 %collective-permute-start.5 = (f32[4,1,128]{2,1,0:T(1,128)S(1)}, f32[4,1,128]{2,1,0:T(1,128)S(1)}, u32[]{:S(2)}, u32[]{:S(2)}) collective-permute-start(f32[4,1,128]{2,1,0:T(1,128)S(1)} %get-tuple-element.41), channel_id=1, source_target_pairs={{0,16},{16,32},{32,48},{48,64},{64,80},{80,96},{96,112},{112,0},{1... | collective-permute-start | bytes 6152 | tf_op jit(solution)/shard_map/ppermute | solution.py:23
  26.1 4.4 %collective-permute-start.7 = (f32[4,128,1]{2,1,0:T(8,128)S(1)}, f32[4,128,1]{2,1,0:T(8,128)S(1)}, u32[]{:S(2)}, u32[]{:S(2)}) collective-permute-start(f32[4,128,1]{2,1,0:T(8,128)S(1)} %get-tuple-element.43), channel_id=1, source_target_pairs={{0,1},{1,2},{2,3},{3,4},{4,5},{5,6},{6,7},{7,8},{8,9},{9,10},{10,1... | collective-permute-start | bytes 6152 | tf_op jit(solution)/shard_map/ppermute | solution.py:23
  33.6 27.0 %all_to_all.28 = bf16[4,128,128]{2,0,1:T(4,128)(2,1)S(1)} all-to-all(bf16[4,128,128]{2,0,1:T(4,128)(2,1)S(1)} %copy.60), channel_id=1, replica_groups=mesh['ox'=8,'oy_0'=2,'oy_1'=4,'oy_2'=2] {'oy_0','oy_1','oy_2'}, dimensions={1} | all-to-all | bytes 262144 | tf_op jit(solution)/shard_map/all_to_all | solution.py:184
  60.8 3.8 %collective-permute-start.9 = (bf16[4,1,2048]{2,0,1:T(4,128)(2,1)S(1)}, bf16[4,1,2048]{2,0,1:T(4,128)(2,1)S(1)}, u32[]{:S(2)}, u32[]{:S(2)}) collective-permute-start(bf16[4,1,2048]{2,0,1:T(4,128)(2,1)S(1)} %get-tuple-element.45), channel_id=1, source_target_pairs={{1,0},{2,1},{3,2},{4,3},{5,4},{6,5},{7,6},{8,7},{9,8},{10,9},{11,1... | collective-permute-start | bytes 49160 | tf_op jit(solution)/shard_map/ppermute | solution.py:40
  67.8 2.8 %fusion.110 = f32[8,2048,64]{1,2,0:T(8,128)} fusion(bf16[4,10,2050]{2,0,1:T(4,128)(2,1)S(1)} %select_maximum_fusion.2, bf16[3,3,64,4]{2,3,1,0:T(4,128)(2,1)S(1)} %copy-done.8), kind=kOutput, calls=%fused_computation.149 | convolution fusion | flops 8388608 | bytes 4326400 | tf_op jit(solution)/shard_map/oc,cxy->oxy/dot_general | solution.py:90
  70.6 2.8 %fusion.112 = f32[8,2048,64]{1,2,0:T(8,128)} fusion(bf16[4,10,2050]{2,0,1:T(4,128)(2,1)S(1)} %select_maximum_fusion.2, bf16[3,3,64,4]{2,3,1,0:T(4,128)(2,1)S(1)} %copy-done.8), kind=kOutput, calls=%fused_computation.151 | convolution fusion | flops 8388608 | bytes 4326400 | tf_op jit(solution)/shard_map/oc,cxy->oxy/dot_general | solution.py:90
  73.4 2.7 %fusion.114 = f32[8,2048,64]{1,2,0:T(8,128)} fusion(bf16[4,10,2050]{2,0,1:T(4,128)(2,1)S(1)} %select_maximum_fusion.2, bf16[3,3,64,4]{2,3,1,0:T(4,128)(2,1)S(1)} %copy-done.8), kind=kOutput, calls=%fused_computation.153 | convolution fusion | flops 8388608 | bytes 4326400 | tf_op jit(solution)/shard_map/oc,cxy->oxy/dot_general | solution.py:90
  76.1 2.7 %fusion.94 = f32[8,2048,64]{1,2,0:T(8,128)} fusion(bf16[4,8,2048]{2,0,1:T(4,128)(2,1)S(1)} %all_to_all.22, bf16[4,1,2048]{2,0,1:T(4,128)(2,1)S(1)} %collective-permute-done.8, bf16[3,3,64,4]{2,3,1,0:T(4,128)(2,1)S(1)} %copy-done.8), kind=kOutput, calls=%fused_computation.135 | convolution fusion | flops 8683520 | bytes 4342784 | tf_op jit(solution)/shard_map/oc,cxy->oxy/dot_general | solution.py:90
  78.8 2.7 %fusion.98 = f32[8,2048,64]{1,2,0:T(8,128)} fusion(bf16[4,1,2048]{2,0,1:T(4,128)(2,1)S(1)} %collective-permute-done.9, bf16[4,8,2048]{2,0,1:T(4,128)(2,1)S(1)} %all_to_all.22, bf16[3,3,64,4]{2,3,1,0:T(4,128)(2,1)S(1)} %copy-done.8), kind=kOutput, calls=%fused_computation.139 | convolution fusion | flops 8683520 | bytes 4342784 | tf_op jit(solution)/shard_map/oc,cxy->oxy/dot_general | solution.py:90
  81.6 9.5 %fusion.7 = bf16[64,8,2048]{2,0,1:T(8,128)(2,1)S(1)} fusion(f32[8,2048,64]{1,2,0:T(8,128)} %fusion.98, f32[8,2048,64]{1,2,0:T(8,128)S(1)} %fusion.106, f32[8,2048,64]{1,2,0:T(8,128)S(1)} %fusion.108, f32[8,2048,64]{1,2,0:T(8,128)S(1)} %fusion.152, f32[8,2048,64]{1,2,0:T(8,128)} %fusion.110, f32[8,2048,64]{1,2,0:T(8,128)} %fusion.112, ...), kind=kOutput, calls=%fused_computation.13 | convolution fusion | flops 23068672 | bytes 35784192 | tf_op jit(solution)/shard_map/oc,cxy->oxy/dot_general | solution.py:90
  91.2 4.1 %collective-permute-start.11 = (bf16[64,1,2048]{2,0,1:T(8,128)(2,1)S(1)}, bf16[64,1,2048]{2,0,1:T(8,128)(2,1)S(1)}, u32[]{:S(2)}, u32[]{:S(2)}) collective-permute-start(bf16[64,1,2048]{2,0,1:T(8,128)(2,1)S(1)} %get-tuple-element.23), channel_id=1, source_target_pairs={{1,0},{2,1},{3,2},{4,3},{5,4},{6,5},{7,6},{8,7},{9,8},{10,9},{11,1... | collective-permute-start | bytes 786440 | tf_op jit(solution)/shard_map/ppermute | solution.py:40
  96.0 3.1 %collective-permute-done.10 = bf16[64,1,2048]{2,0,1:T(8,128)(2,1)S(1)} collective-permute-done((bf16[64,1,2048]{2,0,1:T(8,128)(2,1)S(1)}, bf16[64,1,2048]{2,0,1:T(8,128)(2,1)S(1)}, u32[]{:S(2)}, u32[]{:S(2)}) %collective-permute-start.10) | collective-permute-done | bytes 262176 | tf_op jit(solution)/shard_map/ppermute | solution.py:39
  100.9 2.7 %fusion.38 = f32[8,2048,64]{1,2,0:T(8,128)} fusion(bf16[64,10,2050]{2,0,1:T(8,128)(2,1)S(1)} %fusion.13, bf16[3,3,64,64]{3,2,1,0:T(8,128)(2,1)S(1)} %copy-done.7), kind=kOutput, calls=%fused_computation.47 | convolution fusion | flops 134217728 | bytes 6307840 | tf_op jit(solution)/shard_map/oc,cxy->oxy/dot_general | solution.py:90
  103.6 2.8 %fusion.40 = f32[8,2048,64]{1,2,0:T(8,128)} fusion(bf16[64,10,2050]{2,0,1:T(8,128)(2,1)S(1)} %fusion.13, bf16[3,3,64,64]{3,2,1,0:T(8,128)(2,1)S(1)} %copy-done.7), kind=kOutput, calls=%fused_computation.49 | convolution fusion | flops 134217728 | bytes 6307840 | tf_op jit(solution)/shard_map/oc,cxy->oxy/dot_general | solution.py:90
  109.1 2.8 %fusion.44 = f32[8,2048,64]{1,2,0:T(8,128)} fusion(bf16[64,10,2050]{2,0,1:T(8,128)(2,1)S(1)} %fusion.13, bf16[3,3,64,64]{3,2,1,0:T(8,128)(2,1)S(1)} %copy-done.7), kind=kOutput, calls=%fused_computation.53 | convolution fusion | flops 134217728 | bytes 6307840 | tf_op jit(solution)/shard_map/oc,cxy->oxy/dot_general | solution.py:90
  111.8 2.7 %fusion.48 = f32[8,2048,64]{1,2,0:T(8,128)} fusion(bf16[64,10,2050]{2,0,1:T(8,128)(2,1)S(1)} %fusion.13, bf16[3,3,64,64]{3,2,1,0:T(8,128)(2,1)S(1)} %copy-done.7), kind=kOutput, calls=%fused_computation.58 | convolution fusion | flops 134217728 | bytes 6307840 | tf_op jit(solution)/shard_map/oc,cxy->oxy/dot_general | solution.py:90
  114.5 2.7 %fusion.46 = f32[8,2048,64]{1,2,0:T(8,128)} fusion(bf16[64,8,2048]{2,0,1:T(8,128)(2,1)S(1)} %fusion.7, bf16[64,1,2048]{2,0,1:T(8,128)(2,1)S(1)} %collective-permute-done.10, bf16[3,3,64,64]{3,2,1,0:T(8,128)(2,1)S(1)} %copy-done.7), kind=kOutput, calls=%fused_computation.56 | convolution fusion | flops 138412032 | bytes 6569984 | tf_op jit(solution)/shard_map/oc,cxy->oxy/dot_general | solution.py:90
  117.2 2.7 %fusion.36 = f32[8,2048,64]{1,2,0:T(8,128)} fusion(bf16[64,1,2048]{2,0,1:T(8,128)(2,1)S(1)} %collective-permute-done.11, bf16[64,8,2048]{2,0,1:T(8,128)(2,1)S(1)} %fusion.7, bf16[3,3,64,64]{3,2,1,0:T(8,128)(2,1)S(1)} %copy-done.7), kind=kOutput, calls=%fused_computation.45 | convolution fusion | flops 138412032 | bytes 6569984 | tf_op jit(solution)/shard_map/oc,cxy->oxy/dot_general | solution.py:90
  119.9 10.9 %fusion.8 = bf16[64,8,2048]{2,0,1:T(8,128)(2,1)S(1)} fusion(f32[8,2048,64]{1,2,0:T(8,128)} %fusion.36, f32[8,2048,64]{1,2,0:T(8,128)} %fusion.38, f32[8,2048,64]{1,2,0:T(8,128)} %fusion.40, f32[8,2048,64]{1,2,0:T(8,128)S(1)} %fusion.133, f32[8,2048,64]{1,2,0:T(8,128)} %fusion.42, f32[8,2048,64]{1,2,0:T(8,128)} %fusion.44, f32[8,2048,64]{1,2,0:T(8,128)} %fusion.48, ...), kind=kOutput, calls=%fused_computation.14 | convolution fusion | flops 148897792 | bytes 37765632 | tf_op jit(solution)/shard_map/oc,cxy->oxy/dot_general | solution.py:90
  130.9 4.3 %collective-permute-start.13 = (bf16[64,1,2048]{2,0,1:T(8,128)(2,1)S(1)}, bf16[64,1,2048]{2,0,1:T(8,128)(2,1)S(1)}, u32[]{:S(2)}, u32[]{:S(2)}) collective-permute-start(bf16[64,1,2048]{2,0,1:T(8,128)(2,1)S(1)} %get-tuple-element.21), channel_id=1, source_target_pairs={{1,0},{2,1},{3,2},{4,3},{5,4},{6,5},{7,6},{8,7},{9,8},{10,9},{11,1... | collective-permute-start | bytes 786440 | tf_op jit(solution)/shard_map/ppermute | solution.py:40
  135.7 3.3 %collective-permute-done.12 = bf16[64,1,2048]{2,0,1:T(8,128)(2,1)S(1)} collective-permute-done((bf16[64,1,2048]{2,0,1:T(8,128)(2,1)S(1)}, bf16[64,1,2048]{2,0,1:T(8,128)(2,1)S(1)}, u32[]{:S(2)}, u32[]{:S(2)}) %collective-permute-start.12) | collective-permute-done | bytes 262176 | tf_op jit(solution)/shard_map/ppermute | solution.py:39
  145.8 3.8 %all_to_all.29 = f32[8,2,1,8,128]{4,3,0,2,1:T(8,128)S(1)} all-to-all(f32[8,2,1,8,128]{4,3,0,2,1:T(8,128)S(1)} %copy.62), channel_id=1, replica_groups=mesh['ox'=8,'oy_0'=2,'oy_1'=4,'oy_2'=2] {'oy_2'}, dimensions={1} | all-to-all | bytes 131072 | tf_op jit(solution)/shard_map/all_to_all | solution.py:67
  149.6 23.1 %all_to_all.30 = f32[8,2,1,8,128]{4,3,1,2,0:T(8,128)S(1)} all-to-all(f32[8,2,1,8,128]{4,3,1,2,0:T(8,128)S(1)} %copy.63), channel_id=1, replica_groups=mesh['ox'=8,'oy_0'=2,'oy_1'=4,'oy_2'=2] {'oy_0','oy_1'}, dimensions={0} | all-to-all | bytes 131072 | tf_op jit(solution)/shard_map/all_to_all | solution.py:67
  (100 shorter events, 37.1 us)
Async XLA Ops:
  2.7 9.5 %copy-start.3 = (s32[128,128]{1,0:T(8,128)S(1)}, s32[128,128]{1,0:T(8,128)}, u32[]{:S(2)}) copy-start(s32[128,128]{1,0:T(8,128)} %param.15) | copy-start | bytes 196612
  3.8 12.1 %copy-start = (f32[128,128]{1,0:T(8,128)S(1)}, f32[128,128]{1,0:T(8,128)}, u32[]{:S(2)}) copy-start(f32[128,128]{1,0:T(8,128)} %param.16) | copy-start | bytes 196612
  3.8 12.8 %collective-permute-start = (f32[13,1,128]{2,1,0:T(1,128)S(1)}, f32[13,1,128]{2,1,0:T(1,128)S(1)}, u32[]{:S(2)}, u32[]{:S(2)}) collective-permute-start(f32[13,1,128]{2,1,0:T(1,128)S(1)} %get-tuple-element.30), channel_id=1, source_target_pairs={{16,0},{32,16},{48,32},{64,48},{80,64},{96,80},{112,96},{0,112},{1... | collective-permute-start | bytes 19976 | tf_op jit(solution)/shard_map/ppermute | solution.py:26
  4.4 12.2 %collective-permute-start.1 = (f32[13,1,128]{2,1,0:T(1,128)S(1)}, f32[13,1,128]{2,1,0:T(1,128)S(1)}, u32[]{:S(2)}, u32[]{:S(2)}) collective-permute-start(f32[13,1,128]{2,1,0:T(1,128)S(1)} %get-tuple-element.31), channel_id=1, source_target_pairs={{0,16},{16,32},{32,48},{48,64},{64,80},{80,96},{96,112},{112,0},{1... | collective-permute-start | bytes 19976 | tf_op jit(solution)/shard_map/ppermute | solution.py:23
  8.6 8.2 %copy-start.2 = (f32[4,128,128]{2,1,0:T(8,128)S(1)}, f32[4,128,128]{2,1,0:T(8,128)}, u32[]{:S(2)}) copy-start(f32[4,128,128]{2,1,0:T(8,128)} %param.14) | copy-start | bytes 786436
  8.6 6.9 %collective-permute-start.3 = (f32[13,128,1]{1,2,0:T(1,128)S(1)}, f32[13,128,1]{1,2,0:T(1,128)S(1)}, u32[]{:S(2)}, u32[]{:S(2)}) collective-permute-start(f32[13,128,1]{1,2,0:T(1,128)S(1)} %copy.58), channel_id=1, source_target_pairs={{0,1},{1,2},{2,3},{3,4},{4,5},{5,6},{6,7},{7,8},{8,9},{9,10},{10,1... | collective-permute-start | bytes 19976 | tf_op jit(solution)/shard_map/ppermute | solution.py:23
  10.3 4.9 %collective-permute-start.2 = (f32[13,128,1]{1,2,0:T(1,128)S(1)}, f32[13,128,1]{1,2,0:T(1,128)S(1)}, u32[]{:S(2)}, u32[]{:S(2)}) collective-permute-start(f32[13,128,1]{1,2,0:T(1,128)S(1)} %copy.56), channel_id=1, source_target_pairs={{1,0},{2,1},{3,2},{4,3},{5,4},{6,5},{7,6},{8,7},{9,8},{10,9},{11,1... | collective-permute-start | bytes 19976 | tf_op jit(solution)/shard_map/ppermute | solution.py:26
  17.1 16.3 %copy-start.1 = (f32[4,128,128]{2,1,0:T(8,128)}, f32[4,128,128]{2,1,0:T(8,128)S(1)}, u32[]{:S(2)}) copy-start(f32[4,128,128]{2,1,0:T(8,128)S(1)} %fusion.89) | copy-start | bytes 786436
  20.6 9.9 %collective-permute-start.4 = (f32[4,1,128]{2,1,0:T(1,128)S(1)}, f32[4,1,128]{2,1,0:T(1,128)S(1)}, u32[]{:S(2)}, u32[]{:S(2)}) collective-permute-start(f32[4,1,128]{2,1,0:T(1,128)S(1)} %get-tuple-element.40), channel_id=1, source_target_pairs={{16,0},{32,16},{48,32},{64,48},{80,64},{96,80},{112,96},{0,112},{1... | collective-permute-start | bytes 6152 | tf_op jit(solution)/shard_map/ppermute | solution.py:26
  20.7 9.8 %collective-permute-start.5 = (f32[4,1,128]{2,1,0:T(1,128)S(1)}, f32[4,1,128]{2,1,0:T(1,128)S(1)}, u32[]{:S(2)}, u32[]{:S(2)}) collective-permute-start(f32[4,1,128]{2,1,0:T(1,128)S(1)} %get-tuple-element.41), channel_id=1, source_target_pairs={{0,16},{16,32},{32,48},{48,64},{64,80},{80,96},{96,112},{112,0},{1... | collective-permute-start | bytes 6152 | tf_op jit(solution)/shard_map/ppermute | solution.py:23
  24.8 5.7 %collective-permute-start.6 = (f32[4,128,1]{2,1,0:T(8,128)S(1)}, f32[4,128,1]{2,1,0:T(8,128)S(1)}, u32[]{:S(2)}, u32[]{:S(2)}) collective-permute-start(f32[4,128,1]{2,1,0:T(8,128)S(1)} %get-tuple-element.42), channel_id=1, source_target_pairs={{1,0},{2,1},{3,2},{4,3},{5,4},{6,5},{7,6},{8,7},{9,8},{10,9},{11,1... | collective-permute-start | bytes 6152 | tf_op jit(solution)/shard_map/ppermute | solution.py:26
  26.1 5.5 %collective-permute-start.7 = (f32[4,128,1]{2,1,0:T(8,128)S(1)}, f32[4,128,1]{2,1,0:T(8,128)S(1)}, u32[]{:S(2)}, u32[]{:S(2)}) collective-permute-start(f32[4,128,1]{2,1,0:T(8,128)S(1)} %get-tuple-element.43), channel_id=1, source_target_pairs={{0,1},{1,2},{2,3},{3,4},{4,5},{5,6},{6,7},{7,8},{8,9},{9,10},{10,1... | collective-permute-start | bytes 6152 | tf_op jit(solution)/shard_map/ppermute | solution.py:23
  33.3 27.3 %copy-start.5 = (f32[4,128,128]{2,1,0:T(8,128)}, f32[4,128,128]{2,1,0:T(8,128)S(1)}, u32[]{:S(2)}) copy-start(f32[4,128,128]{2,1,0:T(8,128)S(1)} %get-tuple-element.15) | copy-start | bytes 786436
  33.3 33.7 %copy-start.4 = (f32[4,128,128]{2,1,0:T(8,128)}, f32[4,128,128]{2,1,0:T(8,128)S(1)}, u32[]{:S(2)}) copy-start(f32[4,128,128]{2,1,0:T(8,128)S(1)} %get-tuple-element.14) | copy-start | bytes 786436
  33.4 32.9 %copy-start.8 = (bf16[3,3,64,4]{2,3,1,0:T(4,128)(2,1)S(1)}, bf16[3,3,64,4]{2,3,1,0:T(4,128)(2,1)}, u32[]{:S(2)}) copy-start(bf16[3,3,64,4]{2,3,1,0:T(4,128)(2,1)} %param.19) | copy-start | bytes 13828
  60.7 5.4 %collective-permute-start.8 = (bf16[4,1,2048]{2,0,1:T(4,128)(2,1)S(1)}, bf16[4,1,2048]{2,0,1:T(4,128)(2,1)S(1)}, u32[]{:S(2)}, u32[]{:S(2)}) collective-permute-start(bf16[4,1,2048]{2,0,1:T(4,128)(2,1)S(1)} %get-tuple-element.44), channel_id=1, source_target_pairs={{0,1},{1,2},{2,3},{3,4},{4,5},{5,6},{6,7},{7,8},{8,9},{9,10},{10,1... | collective-permute-start | bytes 49160 | tf_op jit(solution)/shard_map/ppermute | solution.py:39
  60.8 5.3 %collective-permute-start.9 = (bf16[4,1,2048]{2,0,1:T(4,128)(2,1)S(1)}, bf16[4,1,2048]{2,0,1:T(4,128)(2,1)S(1)}, u32[]{:S(2)}, u32[]{:S(2)}) collective-permute-start(bf16[4,1,2048]{2,0,1:T(4,128)(2,1)S(1)} %get-tuple-element.45), channel_id=1, source_target_pairs={{1,0},{2,1},{3,2},{4,3},{5,4},{6,5},{7,6},{8,7},{9,8},{10,9},{11,1... | collective-permute-start | bytes 49160 | tf_op jit(solution)/shard_map/ppermute | solution.py:40
  76.1 5.4 %copy-start.9 = (f32[64]{0:T(128)S(1)}, f32[64]{0:T(128)}, u32[]{:S(2)}) copy-start(f32[64]{0:T(128)} %param.20) | copy-start | bytes 772
  81.5 13.7 %copy-start.7 = (bf16[3,3,64,64]{3,2,1,0:T(8,128)(2,1)S(1)}, bf16[3,3,64,64]{3,2,1,0:T(8,128)(2,1)}, u32[]{:S(2)}) copy-start(bf16[3,3,64,64]{3,2,1,0:T(8,128)(2,1)} %param.21) | copy-start | bytes 221188
  91.1 8.0 %collective-permute-start.10 = (bf16[64,1,2048]{2,0,1:T(8,128)(2,1)S(1)}, bf16[64,1,2048]{2,0,1:T(8,128)(2,1)S(1)}, u32[]{:S(2)}, u32[]{:S(2)}) collective-permute-start(bf16[64,1,2048]{2,0,1:T(8,128)(2,1)S(1)} %get-tuple-element.22), channel_id=1, source_target_pairs={{0,1},{1,2},{2,3},{3,4},{4,5},{5,6},{6,7},{7,8},{8,9},{9,10},{10,1... | collective-permute-start | bytes 786440 | tf_op jit(solution)/shard_map/ppermute | solution.py:39
  91.2 8.0 %collective-permute-start.11 = (bf16[64,1,2048]{2,0,1:T(8,128)(2,1)S(1)}, bf16[64,1,2048]{2,0,1:T(8,128)(2,1)S(1)}, u32[]{:S(2)}, u32[]{:S(2)}) collective-permute-start(bf16[64,1,2048]{2,0,1:T(8,128)(2,1)S(1)} %get-tuple-element.23), channel_id=1, source_target_pairs={{1,0},{2,1},{3,2},{4,3},{5,4},{6,5},{7,6},{8,7},{9,8},{10,9},{11,1... | collective-permute-start | bytes 786440 | tf_op jit(solution)/shard_map/ppermute | solution.py:40
  119.9 15.4 %copy-start.11 = (bf16[3,3,1,64]{3,1,2,0:T(4,128)(2,1)S(1)}, bf16[3,3,1,64]{3,1,2,0:T(4,128)(2,1)}, u32[]{:S(2)}) copy-start(bf16[3,3,1,64]{3,1,2,0:T(4,128)(2,1)} %param.23) | copy-start | bytes 3460
  130.8 8.1 %collective-permute-start.12 = (bf16[64,1,2048]{2,0,1:T(8,128)(2,1)S(1)}, bf16[64,1,2048]{2,0,1:T(8,128)(2,1)S(1)}, u32[]{:S(2)}, u32[]{:S(2)}) collective-permute-start(bf16[64,1,2048]{2,0,1:T(8,128)(2,1)S(1)} %get-tuple-element.20), channel_id=1, source_target_pairs={{0,1},{1,2},{2,3},{3,4},{4,5},{5,6},{6,7},{7,8},{8,9},{9,10},{10,1... | collective-permute-start | bytes 786440 | tf_op jit(solution)/shard_map/ppermute | solution.py:39
  130.9 8.2 %collective-permute-start.13 = (bf16[64,1,2048]{2,0,1:T(8,128)(2,1)S(1)}, bf16[64,1,2048]{2,0,1:T(8,128)(2,1)S(1)}, u32[]{:S(2)}, u32[]{:S(2)}) collective-permute-start(bf16[64,1,2048]{2,0,1:T(8,128)(2,1)S(1)} %get-tuple-element.21), channel_id=1, source_target_pairs={{1,0},{2,1},{3,2},{4,3},{5,4},{6,5},{7,6},{8,7},{9,8},{10,9},{11,1... | collective-permute-start | bytes 786440 | tf_op jit(solution)/shard_map/ppermute | solution.py:40
  (2 other events, 3.5 us)
where the time goes:
time: 174 us; the launch traced here: 173 us
  matrix products  61.9 us (36%)
  blocking collectives  53.9 us (31%)
  starting transfers between devices  29.3 us (17%)
  other arithmetic  14.6 us (8%)
  waiting for transfers between devices  8.95 us (5%)
  local copies, waits for them, and re-layouts  3.64 us (2%)
    dot_general x27, matrix products, conv_valid(): jnp.einsum('oc,cxy->oxy', weight[row_off, col_off], extended[:, row_off:r...  61.9 us
    all_to_all x1, blocking collectives, local(): lax.all_to_all(features, OY, split_axis=1, concat_axis=2, tiled=True)  27 us
    all_to_all x2, blocking collectives, turned_blocks(): out = lax.all_to_all(out, axes[k], k, k, tiled=True)  26.9 us
    ppermute x4, starting transfers between devices, with_halo(): lax.ppermute(lax.slice_in_dim(block, block.shape[dim] - width, None, axis...  13.5 us
    ppermute x3, starting transfers between devices, extended_2(): lax.ppermute(first, axis, [(b, a) for a, b in up])  12.3 us
    ppermute x3, waiting for transfers between devices, extended_2(): lax.ppermute(last, axis, up)  6.41 us
    concatenate x3, other arithmetic, extended_2(): jnp.concatenate([jnp.pad(low, around), x, jnp.pad(high, around)], axis=dim)  3.6 us
  transfers between devices with their start and end apart: 14, of which 6 were waited for; matrix products, arithmetic and copies ran while one was open for 4% of the time, Pallas kernels for 0%

commit v1 on v0

v1 whole, which is shorter than its diff:
```python
import jax
import jax.numpy as jnp
from jax import lax
from jax.experimental import pallas as pl
from jax.experimental.pallas import tpu as pltpu
from jax.sharding import PartitionSpec as P

MESH = pl.DeviceIdType.MESH
F32 = jnp.float32
BF16 = jnp.bfloat16

DT = 0.05
REST = 1.4
DRAG = 0.5
LAYERS = 4
N = 128
HID = 64
FIELDS = 16
SEA, VISC, WIND = 12, 13, 14
EXT = N + 16
PAD = N + 32
WINDOWS = 17
GROUPS = 33
STEP = 3


def exchange_kernel(
    z, v, h, ls, vi, w, xw, xe, nh, sh, own, sea_i, sb, nb, load_sem, send_sem, recv_sem
):
    ox, oy = lax.axis_index("ox"), lax.axis_index("oy")
    nx, ny = lax.axis_size("ox"), lax.axis_size("oy")
    east, west = lax.rem(ox + 1, nx), lax.rem(ox + nx - 1, nx)
    north, south = lax.rem(oy + 1, ny), lax.rem(oy + ny - 1, ny)
    peers = (
        (east, oy), (west, oy), (ox, north), (ox, south),
        (east, north), (east, south), (west, north), (west, south),
    )
    barrier = pltpu.get_barrier_semaphore()
    for peer in peers:
        pl.semaphore_signal(barrier, inc=1, device_id=peer, device_id_type=MESH)
    loads = [
        pltpu.make_async_copy(src, dst, load_sem.at[k])
        for k, (src, dst) in enumerate((
            (z, own.at[0:4]), (v, own.at[4:8]), (h, own.at[8:12]), (ls, sea_i),
            (vi, own.at[VISC]), (w, own.at[WIND : WIND + 2]),
        ))
    ]
    for copy in loads:
        copy.start()
    for copy in loads:
        copy.wait()

    lane = lax.broadcasted_iota(jnp.int32, (8, N), 1)
    low = lax.rem(lane, 16) < 8

    def pack(k, carry):
        rows = pl.ds(pl.multiple_of(8 * k, 8), 8)
        own[SEA, rows, :] = sea_i[rows, :].astype(F32)
        halves = []
        for m in range(2):
            packed = own[8 * m, rows, :]
            for j in range(1, 8):
                moved = pltpu.roll(own[8 * m + j, rows, :], 16 * j, 1)
                packed = jnp.where((lane >= 16 * j - 8) & (lane < 16 * j + 8), moved, packed)
            halves.append(packed)
        sb[rows, :] = jnp.where(low, halves[0], pltpu.roll(halves[1], 8, 1))
        nb[rows, :] = jnp.where(low, pltpu.roll(halves[1], N - 8, 1), halves[0])
        return carry

    lax.fori_loop(0, N // 8, pack, 0)
    pl.semaphore_wait(barrier, 8)

    first, last = pl.ds(0, 8), pl.ds(N - 8, 8)
    moves = (
        (own.at[:, last], xw, (east, oy)),
        (own.at[:, first], xe, (west, oy)),
        (nb, sh.at[8 : 8 + N], (ox, north)),
        (sb, nh.at[8 : 8 + N], (ox, south)),
        (nb.at[last], sh.at[0:8], (east, north)),
        (sb.at[last], nh.at[0:8], (east, south)),
        (nb.at[first], sh.at[N + 8 : EXT], (west, north)),
        (sb.at[first], nh.at[N + 8 : EXT], (west, south)),
    )
    sends = [
        pltpu.make_async_remote_copy(
            src_ref=src, dst_ref=dst, send_sem=send_sem.at[k], recv_sem=recv_sem.at[k],
            device_id=peer, device_id_type=MESH,
        )
        for k, (src, dst, peer) in enumerate(moves)
    ]
    for copy in reversed(sends):
        copy.start()
    for copy in sends:
        copy.wait()


def exchange(z, v, h, ls, vi, w):
    any_spec = pl.BlockSpec(memory_space=pl.ANY)
    strip = jax.ShapeDtypeStruct((FIELDS, 8, N), F32)
    side = jax.ShapeDtypeStruct((EXT, N), F32)
    return pl.pallas_call(
        exchange_kernel,
        out_shape=(strip, strip, side, side),
        in_specs=[any_spec] * 6,
        out_specs=[any_spec] * 4,
        scratch_shapes=[
            pltpu.VMEM((FIELDS, N, N), F32),
            pltpu.VMEM((N, N), jnp.int32),
            pltpu.VMEM((N, N), F32),
            pltpu.VMEM((N, N), F32),
            pltpu.SemaphoreType.DMA((6,)),
            pltpu.SemaphoreType.DMA((8,)),
            pltpu.SemaphoreType.DMA((8,)),
        ],
        compiler_params=pltpu.CompilerParams(collective_id=0, has_side_effects=True),
        name="exchange",
    )(z, v, h, ls, vi, w)


def step_kernel(
    z, v, h, ls, vi, w, xw, xe, nh, sh, grav, first_w, first_b, second_w, second_b, last_w,
    z_out, v_out, h_out, visc_out,
    f0, f1, sea_i, ns, p0, p1, t0, t1, zo, vo, fs, h1, rs, re, load_sem, store_sem,
):
    oy, ny = lax.axis_index("oy"), lax.axis_size("oy")
    mid = pl.ds(16, N)
    loads = [
        pltpu.make_async_copy(src, dst, load_sem.at[k])
        for k, (src, dst) in enumerate((
            (z, f0.at[0:4, mid]), (v, f0.at[4:8, mid]), (h, f0.at[8:12, mid]), (ls, sea_i),
            (vi, f0.at[VISC, mid]), (w, f0.at[WIND : WIND + 2, mid]),
            (xw, f0.at[:, 8:16]), (xe, f0.at[:, N + 16 : N + 24]), (nh, ns.at[0]), (sh, ns.at[1]),
        ))
    ]
    for copy in loads:
        copy.start()

    ones = jnp.ones((8, N), F32)
    for rows in (pl.ds(0, 8), pl.ds(PAD - 8, 8)):
        for k in range(FIELDS):
            f0[k, rows, :] = ones
            f1[k, rows, :] = ones
        for k in range(LAYERS):
            p0[k, rows, :] = ones
            p1[k, rows, :] = ones

    lane = lax.broadcasted_iota(jnp.int32, (8, N), 1)
    low = lax.rem(lane, 16) < 8
    has_north = (oy < ny - 1).astype(F32)
    has_south = (oy > 0).astype(F32)
    inside = jnp.where(lane < N // 2, has_north, has_south)
    first_lane, last_lane = lane == 0, lane == N - 1

    def north(a, b):
        a, b = pltpu.roll(a, N - 1, 1), pltpu.roll(b, N - 1, 1)
        return jnp.where(last_lane, b, a), jnp.where(last_lane, a, b)

    def south(a, b):
        a, b = pltpu.roll(a, 1, 1), pltpu.roll(b, 1, 1)
        return jnp.where(first_lane, b, a), jnp.where(first_lane, a, b)

    for copy in loads:
        copy.wait()

    def centre_sea(k, carry):
        f0[SEA, pl.ds(pl.multiple_of(8 * k + 16, 8), 8), :] = sea_i[
            pl.ds(pl.multiple_of(8 * k, 8), 8), :
        ].astype(F32)
        return carry

    lax.fori_loop(0, N // 8, centre_sea, 0)

    def spread(k, carry):
        rows = pl.ds(pl.multiple_of(8 * k + 8, 8), 8)
        src = pl.ds(pl.multiple_of(8 * k, 8), 8)
        a, b = ns[0, src, :], ns[1, src, :]
        packs = (
            jnp.where(low, a, b),
            jnp.where(low, pltpu.roll(a, N - 8, 1), pltpu.roll(b, 8, 1)),
        )

        def side(field):
            pack, j = packs[field // 8], field % 8
            return pltpu.roll(pack, N - 16 * j, 1) if j else pack

        sea0 = f0[SEA, rows, :]
        sea1 = side(SEA) * inside
        f1[SEA, rows, :] = sea1
        f1[VISC, rows, :] = side(VISC) * inside
        for field in (8, 9, 10, 11, WIND, WIND + 1):
            f1[field, rows, :] = side(field)
        for field in range(8):
            f1[field, rows, :] = side(field) * sea1
            f0[field, rows, :] = f0[field, rows, :] * sea0
        return carry

    lax.fori_loop(0, EXT // 8, spread, 0)

    fields = (f0, f1)
    press = (p0, p1)
    depth = (t0, t1)

    def continuity(k, carry):
        start = 8 * k + 8
        rows = pl.ds(pl.multiple_of(start, 8), 8)
        up, down = pl.ds(start + 1, 8), pl.ds(start - 1, 8)
        seas = [f[SEA, rows, :] for f in fields]
        anomaly = [[], []]
        for l in range(LAYERS):
            thick = [f[8 + l, rows, :] for f in fields]
            fy = [f[4 + l, rows, :] * t for f, t in zip(fields, thick)]
            fn, fso = north(*fy), south(*fy)
            for t, f in enumerate(fields):
                fe = f[l, up, :] * f[8 + l, up, :]
                fw = f[l, down, :] * f[8 + l, down, :]
                diverge = (fe - fw) * 0.5 + (fn[t] - fso[t]) * 0.5
                new = thick[t] - DT * seas[t] * diverge
                depth[t][l, rows, :] = new
                anomaly[t].append(new - REST)
        for t in range(2):
            faces = [anomaly[t][3]]
            for l in (2, 1, 0):
                faces.insert(0, faces[0] + anomaly[t][l])
            total = None
            for l in range(LAYERS):
                term = grav[l] * faces[l]
                total = term if total is None else total + term
                press[t][l, rows, :] = total * inside if t else total
        return carry

    lax.fori_loop(0, EXT // 8, continuity, 0)

    copy_h = pltpu.make_async_copy(t0.at[:, mid], h_out, store_sem.at[0])
    copy_h.start()

    total_rows = N * ny
    base_row = oy * N
    shift = jnp.where(lane < N // 2, N, 0)
    row_ids = (
        (base_row + lane).astype(F32),
        (base_row + lane + jnp.where(lane < N // 2, N, -N)).astype(F32),
    )
    del shift
    coriolis = [0.3 + 1.4 * (r + 0.5) / total_rows for r in row_ids]

    def momentum(k, carry):
        start = 8 * k + 8
        rows = pl.ds(pl.multiple_of(start, 8), 8)
        up, down = pl.ds(start + 1, 8), pl.ds(start - 1, 8)
        seas = [f[SEA, rows, :] for f in fields]
        visc = [f[VISC, rows, :] for f in fields]
        vn, vs = north(*visc), south(*visc)
        coef = []
        for t, f in enumerate(fields):
            coef.append([
                0.5 * (visc[t] + other)
                for other in (f[VISC, up, :], f[VISC, down, :], vn[t], vs[t])
            ])
        kinetic = [None, None]
        column = [None, None]
        top = []
        for l in range(LAYERS):
            zc = [f[l, rows, :] for f in fields]
            vc = [f[4 + l, rows, :] for f in fields]
            pc = [p[l, rows, :] for p in press]
            zn, zs = north(*zc), south(*zc)
            wn, ws = north(*vc), south(*vc)
            pn, ps = north(*pc), south(*pc)
            for t, f in enumerate(fields):
                gx = (press[t][l, up, :] - press[t][l, down, :]) * 0.5
                gy = (pn[t] - ps[t]) * 0.5

                def lap(field, centre, n, s):
                    sides = (f[field, up, :], f[field, down, :], n, s)
                    total = coef[t][0] * (sides[0] - centre)
                    for c, q in zip(coef[t][1:], sides[1:]):
                        total = total + c * (q - centre)
                    return total

                thick = depth[t][l, rows, :]
                fz = coriolis[t] * vc[t] - gx + lap(l, zc[t], zn[t], zs[t])
                fv = -coriolis[t] * zc[t] - gy + lap(4 + l, vc[t], wn[t], ws[t])
                if l == 0:
                    fz = fz + f[WIND, rows, :] / thick
                    fv = fv + f[WIND + 1, rows, :] / thick
                if l == LAYERS - 1:
                    fz = fz - DRAG * zc[t]
                    fv = fv - DRAG * vc[t]
                z_new = seas[t] * (zc[t] + DT * fz)
                v_new = seas[t] * (vc[t] + DT * fv)
                if t == 0:
                    zo[l, rows, :] = z_new
                    vo[l, rows, :] = v_new
                part = thick * (z_new * z_new + v_new * v_new)
                kinetic[t] = part if l == 0 else kinetic[t] + part
                column[t] = thick if l == 0 else column[t] + thick
                if l == 0:
                    top.append([z_new, v_new, seas[t] * (thick - REST)])
        for t in range(2):
            top[t].append(seas[t] * (0.5 * kinetic[t] / column[t]))
        for c in range(4):
            pair = top[0][c], top[1][c]
            for b, both in enumerate((south(*pair), pair, north(*pair))):
                for t in range(2):
                    fs[4 * b + c, t, rows, :] = both[t]
        return carry

    lax.fori_loop(0, EXT // 8, momentum, 0)

    copy_z = pltpu.make_async_copy(zo.at[:, mid], z_out, store_sem.at[1])
    copy_v = pltpu.make_async_copy(vo.at[:, mid], v_out, store_sem.at[2])
    copy_z.start()
    copy_v.start()

    edge_row = lax.broadcasted_iota(jnp.int32, (EXT, N), 0)
    keep = jnp.where(edge_row < N, 1.0, jnp.where(edge_row < N + 8, has_north, has_south)) > 0.5
    half = lax.broadcasted_iota(jnp.int32, (16, 12 * 16), 0) < 8
    weights1 = first_w[...]
    bias1 = first_b[...]
    bias2 = second_b[...]

    def silu_of_half(x):
        return x + x * jnp.tanh(x)

    def first_layer(k, carry):
        rows = pl.ds(pl.multiple_of(8 * k + 8, 8), 16)
        turned = []
        for t in range(2):
            block = fs[:, t, rows, :].reshape(12 * 16, N)
            turned.append(block.T)
        edge = jnp.where(half, turned[1][0:16], turned[1][N - 16 : N])
        left = jnp.concatenate([turned[0], edge], axis=0).astype(BF16)
        for q in range(4):
            out = jnp.dot(left, weights1[:, 128 * q : 128 * q + 128], preferred_element_type=F32)
            out = silu_of_half(out + bias1)
            out = jnp.where(keep, out, 0.0)
            where = (2 * k + q // 2, q % 2)
            h1[(0, *where)] = pltpu.roll(out, 1, 0).astype(BF16)
            h1[(1, *where)] = out.astype(BF16)
            h1[(2, *where)] = pltpu.roll(out, EXT - 1, 0).astype(BF16)
        return carry

    lax.fori_loop(0, WINDOWS, first_layer, 0)

    keep_two = jnp.concatenate([keep, keep], axis=1)

    def second_layer(k, carry):
        g = k * STEP
        parts = []
        for b in range(3):
            for d in range(3):
                block = h1[b, pl.ds(g + d // 2, STEP), d % 2]
                parts.append(block.reshape(STEP * EXT, N))
        left = jnp.concatenate(parts, axis=1)
        out = jnp.dot(left, second_w[...], preferred_element_type=F32)
        for i in range(STEP):
            one = silu_of_half(out[i * EXT : (i + 1) * EXT] + bias2)
            one = jnp.where(keep_two, one, 0.0).astype(BF16)
            sums = lax.dot_general(
                last_w[...], one, (((1,), (1,)), ((), ())), preferred_element_type=F32
            )
            rs[g + i] = sums[0:24, 0:N]
            re[g + i, :, 0:16] = sums[0:24, N:EXT]
        return carry

    lax.fori_loop(0, GROUPS // STEP, second_layer, 0)

    upper = lax.broadcasted_iota(jnp.int32, (8, N), 0) < 4

    def last_layer(k, carry):
        g = 2 * k

        def column_sums(ref, b):
            x, y, zz = (ref[g + i, 8 * b : 8 * b + 8, :] for i in range(3))
            y = pltpu.roll(y, 4, 0)
            return jnp.where(upper, x, y) + jnp.where(upper, y, zz)

        inner = [column_sums(rs, b) for b in range(3)]
        from_south = column_sums(re, 0)
        from_north = column_sums(re, 2)
        low_part = jnp.where(
            first_lane, pltpu.roll(from_south, N - 15, 1), pltpu.roll(inner[0], 1, 1)
        )
        high_part = jnp.where(
            last_lane, pltpu.roll(from_north, N - 1, 1), pltpu.roll(inner[2], N - 1, 1)
        )
        visc_out[pl.ds(pl.multiple_of(8 * k, 8), 8), :] = jnp.exp(low_part + inner[1] + high_part)
        return carry

    lax.fori_loop(0, N // 8, last_layer, 0)
    copy_h.wait()
    copy_z.wait()
    copy_v.wait()


def step(fields, strips, grav, first_w, first_b, second_w, second_b, last_w):
    any_spec = pl.BlockSpec(memory_space=pl.ANY)
    vmem = pl.BlockSpec(memory_space=pltpu.VMEM)
    whole = jax.ShapeDtypeStruct((LAYERS, N, N), F32)
    return pl.pallas_call(
        step_kernel,
        out_shape=(whole, whole, whole, jax.ShapeDtypeStruct((N, N), F32)),
        in_specs=[any_spec] * 10 + [pl.BlockSpec(memory_space=pltpu.SMEM)] + [vmem] * 5,
        out_specs=[any_spec] * 3 + [vmem],
        scratch_shapes=[
            pltpu.VMEM((FIELDS, PAD, N), F32),
            pltpu.VMEM((FIELDS, PAD, N), F32),
            pltpu.VMEM((N, N), jnp.int32),
            pltpu.VMEM((2, EXT, N), F32),
            pltpu.VMEM((LAYERS, PAD, N), F32),
            pltpu.VMEM((LAYERS, PAD, N), F32),
            pltpu.VMEM((LAYERS, PAD, N), F32),
            pltpu.VMEM((LAYERS, PAD, N), F32),
            pltpu.VMEM((LAYERS, PAD, N), F32),
            pltpu.VMEM((LAYERS, PAD, N), F32),
            pltpu.VMEM((12, 2, PAD, N), F32),
            pltpu.VMEM((3, 2 * WINDOWS, 2, EXT, N), BF16),
            pltpu.VMEM((GROUPS, 24, N), F32),
            pltpu.VMEM((GROUPS, 24, N), F32),
            pltpu.SemaphoreType.DMA((10,)),
            pltpu.SemaphoreType.DMA((3,)),
        ],
        compiler_params=pltpu.CompilerParams(vmem_limit_bytes=56 * 2**20),
        name="step",
    )(*fields, *strips, grav, first_w, first_b, second_w, second_b, last_w)


def first_weights(conv, bias):
    taps = jnp.transpose(conv, (1, 3, 0, 2)) * BF16(0.5)
    out = [jnp.pad(taps, ((0, 0), (0, 0), (j + 4, 9 - j), (0, 0))) for j in range(8)]
    matrix = jnp.stack(out, axis=3).reshape(12 * 16, 8 * HID)
    return matrix, jnp.tile(bias * 0.5, 2)[None]


def second_weights(conv, bias):
    taps = jnp.transpose(conv, (1, 0, 3, 2)) * BF16(0.5)
    out = [jnp.pad(taps, ((0, 0), (j, 3 - j), (0, 0), (0, 0))) for j in range(4)]
    matrix = jnp.stack(out, axis=3).reshape(3 * 6 * HID, 4 * HID)
    return matrix, jnp.tile(bias * 0.5, 4)[None]


def last_weights(conv):
    taps = conv[:, :, 0, :]
    zero = jnp.zeros((3, HID), BF16)
    rows = []
    for place in (3, 4, 5, None, None, 0, 1, 2):
        row = []
        for m in range(4):
            a = -1 if place is None else m - place + 2
            row.append(taps[a] if 0 <= a < 3 else zero)
        rows.append(jnp.concatenate(row, axis=1))
    matrix = jnp.stack(rows, axis=1).reshape(24, 4 * HID)
    return jnp.pad(matrix, ((0, 8), (0, 0)))


def local(z, v, h, ls, vi, w, grav, conv1, bias1, conv2, bias2, conv3):
    fields = (z, v, h, ls, vi, w)
    strips = exchange(*fields)
    w1, b1 = first_weights(conv1, bias1)
    w2, b2 = second_weights(conv2, bias2)
    return step(fields, strips, grav, w1, b1, w2, b2, last_weights(conv3))


def solution(mesh):
    block, flat = P(None, "ox", "oy"), P("ox", "oy")
    return jax.shard_map(
        local,
        mesh=mesh,
        in_specs=(block, block, block, flat, flat, block) + (P(),) * 6,
        out_specs=(block, block, block, flat),
        check_vma=False,
    )
```

time: 174 us -> 47.6 us (0.27)
  the two profiles are of different devices: /device:TPU:98 before, /device:TPU:25 now
where the time goes in v1:
time: 47.6 us; the launch traced here: 47.2 us
  Pallas kernels  38.5 us (81%)
  local copies, waits for them, and re-layouts  6.8 us (14%)
  other arithmetic  1.12 us (2%)
  between operations  0.8 us (2%)
    pallas_call x1, Pallas kernels, step(): pl.pallas_call(step_kernel, out_shape=(whole, whole, whole, jax.ShapeDtyp...  25.2 us
    pallas_call x1, Pallas kernels, exchange(): pl.pallas_call(exchange_kernel, out_shape=(strip, strip, side, side), in_...  13.3 us
    reshape x1, local copies, waits for them, and re-layouts, second_weights(): matrix = jnp.stack(out, axis=3).reshape(3 * 6 * HID, 4 * HID)  1.56 us
    another operation x2, local copies, waits for them, and re-layouts, second_weights(): matrix = jnp.stack(out, axis=3).reshape(3 * 6 * HID, 4 * HID)  1.14 us

profile of v1, /device:TPU:25, one launch (start us, length us, event | category | flops | bytes accessed | tf_op | source)
XLA Modules:
  0.0 47.2 jit_solution(15014536715337213888)
XLA Ops:
  0.6 0.0 copy-start
  0.6 0.8 %slice_bitcast_fusion.2 = (bf16[3,64]{1,0:T(4,128)(2,1)S(1)}, bf16[3,64]{1,0:T(4,128)(2,1)S(1)}, bf16[3,64]{1,0:T(4,128)(2,1)S(1)}) fusion(bf16[3,3,1,64]{3,1,2,0:T(4,128)(2,1)} %param.23), kind=kLoop, calls=%fused_computation.23 | loop fusion | bytes 2304 | tf_op jit(solution)/shard_map/squeeze | solution.py:450
  1.4 0.1 maximum_bitcast_fusion.3
  1.6 0.6 %pad.66.last_w = bf16[32,256]{1,0:T(8,128)(2,1)} pad(bf16[24,256]{1,0:T(8,128)(2,1)S(1)} %bitcast.49, bf16[]{:T(256)} %constant.4.clone.1), padding=0_8x0_0 | pad | bytes 28674 | tf_op jit(solution)/shard_map/jit(_pad)/pad | solution.py:453
  2.2 0.7 %multiply_bitcast_fusion.1 = bf16[3,4,3,64]{3,1,0,2:T(4,128)(2,1)S(1)} fusion(bf16[3,3,64,4]{2,3,1,0:T(4,128)(2,1)} %param.19), kind=kLoop, calls=%fused_computation.14 | loop fusion | flops 2304 | bytes 9216 | tf_op jit(solution)/shard_map/mul | solution.py:429
  3.1 0.3 copy.23
  3.4 0.9 %reshape.25.first_w = bf16[192,512]{1,0:T(8,128)(2,1)} reshape(bf16[3,4,16,8,64]{4,3,2,1,0:T(8,128)(2,1)S(1)} %copy.23) | data formatting | bytes 393216 | tf_op jit(solution)/shard_map/reshape | solution.py:431
  4.4 0.0 copy-done
  4.4 0.3 pad_bitcast_fusion.3
  4.6 0.3 pad_maximum_fusion
  5.0 0.9 %copy.24 = bf16[3,6,64,4,64]{4,3,2,1,0:T(4,128)(2,1)S(1)} copy(bf16[3,6,64,4,64]{2,4,0,1,3:T(8,128)(2,1)S(1)} %pad_maximum_fusion) | data formatting | bytes 1179648 | tf_op jit(solution)/shard_map/stack | solution.py:438
  5.8 0.0 copy-start.1
  5.9 0.0 copy-start.2
  5.9 1.6 %reshape.26.second_w = bf16[1152,256]{1,0:T(8,128)(2,1)} reshape(bf16[3,6,64,4,64]{4,3,2,1,0:T(4,128)(2,1)S(1)} %copy.24) | data formatting | bytes 1179648 | tf_op jit(solution)/shard_map/reshape | solution.py:438
  7.4 13.3 %exchange.1 = (f32[16,8,128]{2,1,0:T(8,128)}, f32[16,8,128]{2,1,0:T(8,128)}, f32[144,128]{1,0:T(8,128)}, f32[144,128]{1,0:T(8,128)}) custom-call(f32[4,128,128]{2,1,0:T(8,128)} %z.3, f32[4,128,128]{2,1,0:T(8,128)} %v.3, f32[4,128,128]{2,1,0:T(8,128)} %h.3, s32[128,128]{1,0:T(8,128)} %ls.3, f32[128,128]{1,0:T(8,128)} %vi.3, f32[2,128,128]{2,1,0:T(8,128)} %w.3), custom_call_target="tpu_custom_call" | custom-call | tf_op jit(solution)/shard_map/exchange/pallas_call | solution.py:101
  20.7 0.0 copy-done.1
  20.7 0.6 %broadcast_in_dim_tile.7.second_b = f32[1,256]{1,0:T(1,128)} reshape(f32[4,64]{1,0:T(4,128)S(1)} %tile.5) | data formatting | bytes 2048 | tf_op jit(solution)/shard_map/broadcast_in_dim;tile | solution.py:439
  21.4 0.0 copy-done.2
  21.4 0.6 %broadcast_in_dim_tile.6.first_b = f32[1,128]{1,0:T(1,128)} reshape(f32[2,64]{1,0:T(2,128)S(1)} %tile.4) | data formatting | bytes 1024 | tf_op jit(solution)/shard_map/broadcast_in_dim;tile | solution.py:432
  22.0 25.2 %step.1 = (f32[4,128,128]{2,1,0:T(8,128)}, f32[4,128,128]{2,1,0:T(8,128)}, f32[4,128,128]{2,1,0:T(8,128)}, f32[128,128]{1,0:T(8,128)}) custom-call(f32[4,128,128]{2,1,0:T(8,128)} %z.3, f32[4,128,128]{2,1,0:T(8,128)} %v.3, f32[4,128,128]{2,1,0:T(8,128)} %h.3, s32[128,128]{1,0:T(8,128)} %ls.3, f32[128,128]{1,0:T(8,128)} %vi.3, f32[2,128,128]{2,1,0:T(8,128)} %w.3, ...), custom_call_target="tpu_custom_call" | custom-call | tf_op jit(solution)/shard_map/step/pallas_call | solution.py:400
  (23 shorter events, 0.3 us)
Async XLA Ops:
  0.6 3.7 %copy-start = (bf16[3,3,64,64]{3,2,1,0:T(8,128)(2,1)S(1)}, bf16[3,3,64,64]{3,2,1,0:T(8,128)(2,1)}, u32[]{:S(2)}) copy-start(bf16[3,3,64,64]{3,2,1,0:T(8,128)(2,1)} %param.21) | copy-start | bytes 221188
  5.8 14.9 %copy-start.1 = (f32[64]{0:T(128)S(1)}, f32[64]{0:T(128)}, u32[]{:S(2)}) copy-start(f32[64]{0:T(128)} %param.22) | copy-start | bytes 772
  5.9 15.5 %copy-start.2 = (f32[64]{0:T(128)S(1)}, f32[64]{0:T(128)}, u32[]{:S(2)}) copy-start(f32[64]{0:T(128)} %param.20) | copy-start | bytes 772

commit v2 on v1

--- a/solution.py
+++ b/solution.py
@@ -19,9 +19,12 @@
 SEA, VISC, WIND = 12, 13, 14
 EXT = N + 16
 PAD = N + 32
-WINDOWS = 17
+TALL = N + 40
+PAIRS = 72
 GROUPS = 33
 STEP = 3
+TILES = EXT // 16
+BLOCK = STEP * EXT
 
 
 def exchange_kernel(
@@ -117,10 +120,67 @@
     )(z, v, h, ls, vi, w)
 
 
+def build_weights(conv1, conv2, conv3, first_w, second_w, last_w, rows24):
+    lane = lax.broadcasted_iota(jnp.int32, (8, N), 1)
+    right = lane >= HID
+    row = lax.broadcasted_iota(jnp.int32, (8, N), 0)
+
+    scale = lax.broadcasted_iota(jnp.int32, (16, 4), 0) == lax.broadcasted_iota(jnp.int32, (16, 4), 1)
+    scale = jnp.where(scale, 0.5, 0.0).astype(BF16)
+    nt = (((1,), (1,)), ((), ()))
+    taps = {}
+    for a in range(3):
+        for b in range(3):
+            one = conv1[a, b]
+            both = jnp.concatenate([one, one], axis=0)
+            taps[a, b] = lax.dot_general(scale, both, nt, preferred_element_type=F32)
+    for b in range(3):
+        for c in range(4):
+            vecs = [jnp.broadcast_to(taps[a, b][c : c + 1], (8, N)) for a in range(3)]
+            for jp in range(8):
+                parts = []
+                for i in range(4):
+                    gap = row + 8 * i - 2 * jp - jnp.where(right, 1, 0) - 4
+                    val = jnp.zeros((8, N), F32)
+                    for a in range(3):
+                        val = jnp.where(gap == a, vecs[a], val)
+                    parts.append(val)
+                start = 128 * b + 32 * c
+                first_w[start : start + 32, N * jp : N * jp + N] = jnp.concatenate(parts, 0).astype(BF16)
+
+    eye = lax.broadcasted_iota(jnp.int32, (HID, HID), 0) == lax.broadcasted_iota(jnp.int32, (HID, HID), 1)
+    eye = jnp.where(eye, 0.5, 0.0).astype(BF16)
+    side = lax.broadcasted_iota(jnp.int32, (HID, N), 1) >= HID
+    for b in range(3):
+        turned = []
+        for a in range(3):
+            one = conv2[a, b]
+            both = jnp.concatenate([one, one], axis=0)
+            turned.append(lax.dot_general(eye, both, nt, preferred_element_type=F32))
+        zero = jnp.zeros((HID, N), F32)
+        for m in range(6):
+            for jp in range(2):
+                tap = m - 2 * jp
+                left = turned[tap] if 0 <= tap < 3 else zero
+                other = turned[tap - 1] if 0 <= tap - 1 < 3 else zero
+                start = (6 * b + m) * HID
+                second_w[start : start + HID, N * jp : N * jp + N] = jnp.where(side, other, left).astype(BF16)
+
+    rows24[...] = jnp.zeros((32, 2 * N), F32)
+    for b in range(3):
+        for place, i in ((0, 3), (1, 4), (2, 5), (5, 0), (6, 1), (7, 2)):
+            for m in range(4):
+                a = m - i + 2
+                if 0 <= a < 3:
+                    rows24[8 * b + place : 8 * b + place + 1, HID * m : HID * m + HID] = conv3[a, b].astype(F32)
+    last_w[...] = rows24[...].astype(BF16)
+
+
 def step_kernel(
-    z, v, h, ls, vi, w, xw, xe, nh, sh, grav, first_w, first_b, second_w, second_b, last_w,
+    z, v, h, ls, vi, w, xw, xe, nh, sh, grav, conv1, bias1, conv2, bias2, conv3,
     z_out, v_out, h_out, visc_out,
-    f0, f1, sea_i, ns, p0, p1, t0, t1, zo, vo, fs, h1, rs, re, load_sem, store_sem,
+    f0, f1, sea_i, ns, p0, p1, t0, t1, zo, vo, fs, ft, h1, d0, d1, rs, re, nat,
+    first_w, second_w, last_w, rows24, load_sem, store_sem,
 ):
     oy, ny = lax.axis_index("oy"), lax.axis_size("oy")
     mid = pl.ds(16, N)
@@ -143,36 +203,39 @@
         for k in range(LAYERS):
             p0[k, rows, :] = ones
             p1[k, rows, :] = ones
-
-    lane = lax.broadcasted_iota(jnp.int32, (8, N), 1)
-    low = lax.rem(lane, 16) < 8
+    for c in range(4):
+        for t in range(2):
+            fs[c, t, EXT + 8 : TALL, :] = jnp.zeros((TALL - EXT - 8, N), F32)
+    build_weights(conv1, conv2, conv3, first_w, second_w, last_w, rows24)
+
     has_north = (oy < ny - 1).astype(F32)
     has_south = (oy > 0).astype(F32)
-    inside = jnp.where(lane < N // 2, has_north, has_south)
-    first_lane, last_lane = lane == 0, lane == N - 1
+
+    for copy in loads:
+        copy.wait()
+
+    def lanes(rows):
+        return lax.broadcasted_iota(jnp.int32, (rows, N), 1)
 
     def north(a, b):
+        last_lane = lanes(a.shape[0]) == N - 1
         a, b = pltpu.roll(a, N - 1, 1), pltpu.roll(b, N - 1, 1)
         return jnp.where(last_lane, b, a), jnp.where(last_lane, a, b)
 
     def south(a, b):
+        first_lane = lanes(a.shape[0]) == 0
         a, b = pltpu.roll(a, 1, 1), pltpu.roll(b, 1, 1)
         return jnp.where(first_lane, b, a), jnp.where(first_lane, a, b)
 
-    for copy in loads:
-        copy.wait()
-
-    def centre_sea(k, carry):
-        f0[SEA, pl.ds(pl.multiple_of(8 * k + 16, 8), 8), :] = sea_i[
-            pl.ds(pl.multiple_of(8 * k, 8), 8), :
-        ].astype(F32)
-        return carry
-
-    lax.fori_loop(0, N // 8, centre_sea, 0)
+    f0[SEA, mid, :] = sea_i[...].astype(F32)
 
     def spread(k, carry):
-        rows = pl.ds(pl.multiple_of(8 * k + 8, 8), 8)
-        src = pl.ds(pl.multiple_of(8 * k, 8), 8)
+        size = SPREAD
+        lane = lanes(size)
+        low = lax.rem(lane, 16) < 8
+        inside = jnp.where(lane < N // 2, has_north, has_south)
+        rows = pl.ds(pl.multiple_of(size * k + 8, 8), size)
+        src = pl.ds(pl.multiple_of(size * k, 8), size)
         a, b = ns[0, src, :], ns[1, src, :]
         packs = (
             jnp.where(low, a, b),
@@ -194,16 +257,18 @@
             f0[field, rows, :] = f0[field, rows, :] * sea0
         return carry
 
-    lax.fori_loop(0, EXT // 8, spread, 0)
+    lax.fori_loop(0, EXT // SPREAD, spread, 0)
 
     fields = (f0, f1)
     press = (p0, p1)
     depth = (t0, t1)
 
     def continuity(k, carry):
-        start = 8 * k + 8
-        rows = pl.ds(pl.multiple_of(start, 8), 8)
-        up, down = pl.ds(start + 1, 8), pl.ds(start - 1, 8)
+        size = CONT
+        inside = jnp.where(lanes(size) < N // 2, has_north, has_south)
+        start = size * k + 8
+        rows = pl.ds(pl.multiple_of(start, 8), size)
+        up, down = pl.ds(start + 1, size), pl.ds(start - 1, size)
         seas = [f[SEA, rows, :] for f in fields]
         anomaly = [[], []]
         for l in range(LAYERS):
@@ -228,25 +293,25 @@
                 press[t][l, rows, :] = total * inside if t else total
         return carry
 
-    lax.fori_loop(0, EXT // 8, continuity, 0)
+    lax.fori_loop(0, EXT // CONT, continuity, 0)
 
     copy_h = pltpu.make_async_copy(t0.at[:, mid], h_out, store_sem.at[0])
     copy_h.start()
 
     total_rows = N * ny
     base_row = oy * N
-    shift = jnp.where(lane < N // 2, N, 0)
-    row_ids = (
-        (base_row + lane).astype(F32),
-        (base_row + lane + jnp.where(lane < N // 2, N, -N)).astype(F32),
-    )
-    del shift
-    coriolis = [0.3 + 1.4 * (r + 0.5) / total_rows for r in row_ids]
 
     def momentum(k, carry):
-        start = 8 * k + 8
-        rows = pl.ds(pl.multiple_of(start, 8), 8)
-        up, down = pl.ds(start + 1, 8), pl.ds(start - 1, 8)
+        size = MOM
+        lane = lanes(size)
+        start = size * k + 8
+        rows = pl.ds(pl.multiple_of(start, 8), size)
+        up, down = pl.ds(start + 1, size), pl.ds(start - 1, size)
+        row_ids = (
+            (base_row + lane).astype(F32),
+            (base_row + lane + jnp.where(lane < N // 2, N, -N)).astype(F32),
+        )
+        coriolis = [0.3 + 1.4 * (r + 0.5) / total_rows for r in row_ids]
         seas = [f[SEA, rows, :] for f in fields]
         visc = [f[VISC, rows, :] for f in fields]
         vn, vs = north(*visc), south(*visc)
@@ -258,7 +323,6 @@
             ])
         kinetic = [None, None]
         column = [None, None]
-        top = []
         for l in range(LAYERS):
             zc = [f[l, rows, :] for f in fields]
             vc = [f[4 + l, rows, :] for f in fields]
@@ -295,105 +359,125 @@
                 kinetic[t] = part if l == 0 else kinetic[t] + part
                 column[t] = thick if l == 0 else column[t] + thick
                 if l == 0:
-                    top.append([z_new, v_new, seas[t] * (thick - REST)])
+                    fs[0, t, rows, :] = z_new
+                    fs[1, t, rows, :] = v_new
+                    fs[2, t, rows, :] = seas[t] * (thick - REST)
         for t in range(2):
-            top[t].append(seas[t] * (0.5 * kinetic[t] / column[t]))
-        for c in range(4):
-            pair = top[0][c], top[1][c]
-            for b, both in enumerate((south(*pair), pair, north(*pair))):
-                for t in range(2):
-                    fs[4 * b + c, t, rows, :] = both[t]
-        return carry
-
-    lax.fori_loop(0, EXT // 8, momentum, 0)
+            fs[3, t, rows, :] = seas[t] * (0.5 * kinetic[t] / column[t])
+        return carry
+
+    lax.fori_loop(0, EXT // MOM, momentum, 0)
 
     copy_z = pltpu.make_async_copy(zo.at[:, mid], z_out, store_sem.at[1])
     copy_v = pltpu.make_async_copy(vo.at[:, mid], v_out, store_sem.at[2])
     copy_z.start()
     copy_v.start()
 
-    edge_row = lax.broadcasted_iota(jnp.int32, (EXT, N), 0)
-    keep = jnp.where(edge_row < N, 1.0, jnp.where(edge_row < N + 8, has_north, has_south)) > 0.5
-    half = lax.broadcasted_iota(jnp.int32, (16, 12 * 16), 0) < 8
-    weights1 = first_w[...]
-    bias1 = first_b[...]
-    bias2 = second_b[...]
-
-    def silu_of_half(x):
-        return x + x * jnp.tanh(x)
-
-    def first_layer(k, carry):
-        rows = pl.ds(pl.multiple_of(8 * k + 8, 8), 16)
-        turned = []
-        for t in range(2):
-            block = fs[:, t, rows, :].reshape(12 * 16, N)
-            turned.append(block.T)
-        edge = jnp.where(half, turned[1][0:16], turned[1][N - 16 : N])
-        left = jnp.concatenate([turned[0], edge], axis=0).astype(BF16)
-        for q in range(4):
-            out = jnp.dot(left, weights1[:, 128 * q : 128 * q + 128], preferred_element_type=F32)
-            out = silu_of_half(out + bias1)
-            out = jnp.where(keep, out, 0.0)
-            where = (2 * k + q // 2, q % 2)
-            h1[(0, *where)] = pltpu.roll(out, 1, 0).astype(BF16)
-            h1[(1, *where)] = out.astype(BF16)
-            h1[(2, *where)] = pltpu.roll(out, EXT - 1, 0).astype(BF16)
-        return carry
-
-    lax.fori_loop(0, WINDOWS, first_layer, 0)
-
-    keep_two = jnp.concatenate([keep, keep], axis=1)
-
-    def second_layer(k, carry):
+    def turn(k, carry):
+        rows = pl.ds(pl.multiple_of(16 * k + 8, 8), 32)
+        blocks = [fs[:, t, rows, :].reshape(N, N).T for t in range(2)]
+        ft[k, 8 : N + 8, :] = blocks[0]
+        ft[k, N + 8 : N + 16, :] = blocks[1][0:8]
+        ft[k, N + 16 : N + 24, :] = blocks[1][N - 8 : N]
+        ft[k, 0:8, :] = blocks[1][N - 8 : N]
+        ft[k, N + 24 : N + 32, :] = blocks[0][0:8]
+        return carry
+
+    lax.fori_loop(0, 9, turn, 0)
+
+    order = lax.broadcasted_iota(jnp.int32, (EXT, 2 * N), 0)
+    lat = 9 * lax.rem(order, 16) + order // 16
+    keep = jnp.where(lat < N, 1.0, jnp.where(lat < N + 8, has_north, has_south)) > 0.5
+    b1 = jnp.concatenate([bias1[...].reshape(1, HID) * 0.5] * 4, axis=1)
+    b2 = jnp.concatenate([bias2[...].reshape(1, HID) * 0.5] * 4, axis=1)
+
+    def activate(x, bias):
+        x = x + bias
+        return jnp.where(keep, x + x * jnp.tanh(x), 0.0)
+
+    def first_layer(k, quarters):
+        parts = []
+        for b in range(3):
+            pieces = []
+            for t in range(TILES):
+                for half in range(2):
+                    pieces.append(ft[k, pl.ds(7 + t + b + 72 * half, 8, stride=9), :])
+            parts.append(jnp.concatenate(pieces, axis=0).astype(BF16))
+        left = jnp.concatenate(parts, axis=1)
+        for q in range(quarters):
+            out = jnp.dot(left, first_w[:, 256 * q : 256 * q + 256], preferred_element_type=F32)
+            out = activate(out, b1)
+            for p in range(2):
+                one = out[:, N * p : N * p + N]
+                h1[4 * k + q, p, 16 : 16 + EXT, :] = one.astype(BF16)
+                h1[4 * k + q, p, 0:16, :] = pltpu.roll(one[EXT - 16 : EXT], 1, 0).astype(BF16)
+                h1[4 * k + q, p, 16 + EXT : 32 + EXT, :] = pltpu.roll(one[0:16], 15, 0).astype(BF16)
+
+    def first_body(k, carry):
+        first_layer(k, 4)
+        return carry
+
+    lax.fori_loop(0, 8, first_body, 0)
+    first_layer(8, 2)
+
+    def second_matmul(k, ref):
         g = k * STEP
         parts = []
         for b in range(3):
             for d in range(3):
-                block = h1[b, pl.ds(g + d // 2, STEP), d % 2]
-                parts.append(block.reshape(STEP * EXT, N))
+                block = h1[pl.ds(g + d // 2, STEP), d % 2, 16 * b : 16 * b + EXT, :]
+                parts.append(block.reshape(BLOCK, N))
         left = jnp.concatenate(parts, axis=1)
-        out = jnp.dot(left, second_w[...], preferred_element_type=F32)
+        ref[...] = jnp.dot(left, second_w[...], preferred_element_type=F32)
+
+    def finish(k, ref):
         for i in range(STEP):
-            one = silu_of_half(out[i * EXT : (i + 1) * EXT] + bias2)
-            one = jnp.where(keep_two, one, 0.0).astype(BF16)
+            one = activate(ref[i * EXT : (i + 1) * EXT], b2).astype(BF16)
             sums = lax.dot_general(
                 last_w[...], one, (((1,), (1,)), ((), ())), preferred_element_type=F32
             )
-            rs[g + i] = sums[0:24, 0:N]
-            re[g + i, :, 0:16] = sums[0:24, N:EXT]
-        return carry
-
-    lax.fori_loop(0, GROUPS // STEP, second_layer, 0)
+            rs[k * STEP + i] = sums[0:24, 0:N]
+            re[k * STEP + i, :, 0:16] = sums[0:24, N:EXT]
+
+    second_matmul(0, d0)
+
+    def second_layer(k, carry):
+        second_matmul(2 * k + 1, d1)
+        finish(2 * k, d0)
+        second_matmul(2 * k + 2, d0)
+        finish(2 * k + 1, d1)
+        return carry
+
+    lax.fori_loop(0, 5, second_layer, 0)
+    finish(10, d0)
 
     upper = lax.broadcasted_iota(jnp.int32, (8, N), 0) < 4
-
-    def last_layer(k, carry):
-        g = 2 * k
-
-        def column_sums(ref, b):
-            x, y, zz = (ref[g + i, 8 * b : 8 * b + 8, :] for i in range(3))
-            y = pltpu.roll(y, 4, 0)
-            return jnp.where(upper, x, y) + jnp.where(upper, y, zz)
-
-        inner = [column_sums(rs, b) for b in range(3)]
-        from_south = column_sums(re, 0)
-        from_north = column_sums(re, 2)
-        low_part = jnp.where(
-            first_lane, pltpu.roll(from_south, N - 15, 1), pltpu.roll(inner[0], 1, 1)
-        )
-        high_part = jnp.where(
-            last_lane, pltpu.roll(from_north, N - 1, 1), pltpu.roll(inner[2], N - 1, 1)
-        )
-        visc_out[pl.ds(pl.multiple_of(8 * k, 8), 8), :] = jnp.exp(low_part + inner[1] + high_part)
-        return carry
-
-    lax.fori_loop(0, N // 8, last_layer, 0)
+    for b in range(3):
+        blocks = []
+        for ref in (rs, re):
+            rows = []
+            for k in range(N // 8):
+                x, y, zz = (ref[2 * k + i, 8 * b : 8 * b + 8, :] for i in range(3))
+                y = pltpu.roll(y, 4, 0)
+                rows.append(jnp.where(upper, x, y) + jnp.where(upper, y, zz))
+            blocks.append(jnp.concatenate(rows, axis=0).T)
+        for t in range(TILES):
+            for half in range(2):
+                block, at = (blocks[0], 16 * t) if t < 8 else (blocks[1], 0)
+                at = at + 8 * half
+                nat[b, pl.ds(8 + t + 72 * half, 8, stride=9), :] = block[at : at + 8]
+        nat[b, 0:8, :] = nat[b, EXT : EXT + 8, :]
+    total = nat[0, 7 : 7 + N, :] + nat[1, 8 : 8 + N, :] + nat[2, 9 : 9 + N, :]
+    visc_out[...] = jnp.exp(total.T)
     copy_h.wait()
     copy_z.wait()
     copy_v.wait()
 
 
-def step(fields, strips, grav, first_w, first_b, second_w, second_b, last_w):
+SPREAD, CONT, MOM = 48, 24, 16
+
+
+def step(fields, strips, grav, conv1, bias1, conv2, bias2, conv3):
     any_spec = pl.BlockSpec(memory_space=pl.ANY)
     vmem = pl.BlockSpec(memory_space=pltpu.VMEM)
     whole = jax.ShapeDtypeStruct((LAYERS, N, N), F32)
@@ -413,52 +497,30 @@
             pltpu.VMEM((LAYERS, PAD, N), F32),
             pltpu.VMEM((LAYERS, PAD, N), F32),
             pltpu.VMEM((LAYERS, PAD, N), F32),
-            pltpu.VMEM((12, 2, PAD, N), F32),
-            pltpu.VMEM((3, 2 * WINDOWS, 2, EXT, N), BF16),
+            pltpu.VMEM((4, 2, TALL, N), F32),
+            pltpu.VMEM((9, EXT + 16, N), F32),
+            pltpu.VMEM((PAIRS // 2, 2, EXT + 32, N), BF16),
+            pltpu.VMEM((BLOCK, 2 * N), F32),
+            pltpu.VMEM((BLOCK, 2 * N), F32),
             pltpu.VMEM((GROUPS, 24, N), F32),
             pltpu.VMEM((GROUPS, 24, N), F32),
+            pltpu.VMEM((3, EXT + 16, N), F32),
+            pltpu.VMEM((3 * N, 16 * HID), BF16),
+            pltpu.VMEM((18 * HID, 4 * HID), BF16),
+            pltpu.VMEM((32, 2 * N), BF16),
+            pltpu.VMEM((32, 2 * N), F32),
             pltpu.SemaphoreType.DMA((10,)),
             pltpu.SemaphoreType.DMA((3,)),
         ],
         compiler_params=pltpu.CompilerParams(vmem_limit_bytes=56 * 2**20),
         name="step",
-    )(*fields, *strips, grav, first_w, first_b, second_w, second_b, last_w)
-
-
-def first_weights(conv, bias):
-    taps = jnp.transpose(conv, (1, 3, 0, 2)) * BF16(0.5)
-    out = [jnp.pad(taps, ((0, 0), (0, 0), (j + 4, 9 - j), (0, 0))) for j in range(8)]
-    matrix = jnp.stack(out, axis=3).reshape(12 * 16, 8 * HID)
-    return matrix, jnp.tile(bias * 0.5, 2)[None]
-
-
-def second_weights(conv, bias):
-    taps = jnp.transpose(conv, (1, 0, 3, 2)) * BF16(0.5)
-    out = [jnp.pad(taps, ((0, 0), (j, 3 - j), (0, 0), (0, 0))) for j in range(4)]
-    matrix = jnp.stack(out, axis=3).reshape(3 * 6 * HID, 4 * HID)
-    return matrix, jnp.tile(bias * 0.5, 4)[None]
-
-
-def last_weights(conv):
-    taps = conv[:, :, 0, :]
-    zero = jnp.zeros((3, HID), BF16)
-    rows = []
-    for place in (3, 4, 5, None, None, 0, 1, 2):
-        row = []
-        for m in range(4):
-            a = -1 if place is None else m - place + 2
-            row.append(taps[a] if 0 <= a < 3 else zero)
-        rows.append(jnp.concatenate(row, axis=1))
-    matrix = jnp.stack(rows, axis=1).reshape(24, 4 * HID)
-    return jnp.pad(matrix, ((0, 8), (0, 0)))
+    )(*fields, *strips, grav, conv1, bias1, conv2, bias2, conv3)
 
 
 def local(z, v, h, ls, vi, w, grav, conv1, bias1, conv2, bias2, conv3):
     fields = (z, v, h, ls, vi, w)
     strips = exchange(*fields)
-    w1, b1 = first_weights(conv1, bias1)
-    w2, b2 = second_weights(conv2, bias2)
-    return step(fields, strips, grav, w1, b1, w2, b2, last_weights(conv3))
+    return step(fields, strips, grav, conv1, bias1, conv2, bias2, conv3)
 
 
 def solution(mesh):

time: 47.6 us -> 32.6 us (0.68)
  Pallas kernels: 38.5 us -> 28.8 us
  local copies, waits for them, and re-layouts: 6.8 us -> 2.77 us
  other arithmetic: 1.12 us -> 0 us
    pallas_call x1, Pallas kernels: 25.2 us -> 15.5 us  [step(): pl.pallas_call(step_kernel, out_shape=(whole, whole, whole, jax.ShapeDtyp...]
    another operation x17 -> x0, local copies, waits for them, and re-layouts: 2.75 us -> none  [the longest x2 1.14 us: second_weights(): matrix = jnp.stack(out, axis=3).reshape(3 * 6 * HID, 4 * HID)]
    unnamed x13 -> x2, local copies, waits for them, and re-layouts: 0.19 us -> 2.77 us
    reshape x2 -> x0, local copies, waits for them, and re-layouts: 2.5 us -> none  [the longest x1 1.56 us: second_weights(): matrix = jnp.stack(out, axis=3).reshape(3 * 6 * HID, 4 * HID)]
    squeeze x1 -> x0, local copies, waits for them, and re-layouts: 0.75 us -> none  [last_weights(): row.append(taps[a] if 0 <= a < 3 else zero)]
    mul x4 -> x0, other arithmetic: 0.73 us -> none  [the longest x1 0.71 us: first_weights(): taps = jnp.transpose(conv, (1, 3, 0, 2)) * BF16(0.5)]
    pad x1 -> x0, local copies, waits for them, and re-layouts: 0.6 us -> none  [last_weights(): return jnp.pad(matrix, ((0, 8), (0, 0)))]
where the time goes in v2:
time: 32.6 us; the launch traced here: 32.2 us
  Pallas kernels  28.8 us (88%)
  local copies, waits for them, and re-layouts  2.77 us (8%)
  between operations  0.64 us (2%)
    pallas_call x1, Pallas kernels, step(): pl.pallas_call(step_kernel, out_shape=(whole, whole, whole, jax.ShapeDtyp...  15.5 us
    pallas_call x1, Pallas kernels, exchange(): pl.pallas_call(exchange_kernel, out_shape=(strip, strip, side, side), in_...  13.3 us
    unnamed x2, local copies, waits for them, and re-layouts  2.77 us

profile of v2, /device:TPU:25, one launch (start us, length us, event | category | flops | bytes accessed | tf_op | source)
XLA Modules:
  0.0 32.2 jit_solution(16196068159098125759)
XLA Ops:
  0.6 1.3 %copy.17.conv3 = bf16[3,3,1,64]{3,2,1,0:T(2,128)(2,1)} copy(bf16[3,3,1,64]{3,1,2,0:T(4,128)(2,1)} %param.23) | data formatting | bytes 2304 | tf_op args[11]
  1.9 1.5 %copy.16.conv1 = bf16[3,3,64,4]{3,2,1,0:T(8,128)(2,1)} copy(bf16[3,3,64,4]{2,3,1,0:T(4,128)(2,1)} %param.19) | data formatting | bytes 9216 | tf_op args[7]
  3.4 13.3 %exchange.1 = (f32[16,8,128]{2,1,0:T(8,128)}, f32[16,8,128]{2,1,0:T(8,128)}, f32[144,128]{1,0:T(8,128)}, f32[144,128]{1,0:T(8,128)}) custom-call(f32[4,128,128]{2,1,0:T(8,128)} %z.3, f32[4,128,128]{2,1,0:T(8,128)} %v.3, f32[4,128,128]{2,1,0:T(8,128)} %h.3, s32[128,128]{1,0:T(8,128)} %ls.3, f32[128,128]{1,0:T(8,128)} %vi.3, f32[2,128,128]{2,1,0:T(8,128)} %w.3), custom_call_target="tpu_custom_call" | custom-call | tf_op jit(solution)/shard_map/exchange/pallas_call | solution.py:104
  16.7 15.5 %step.1 = (f32[4,128,128]{2,1,0:T(8,128)}, f32[4,128,128]{2,1,0:T(8,128)}, f32[4,128,128]{2,1,0:T(8,128)}, f32[128,128]{1,0:T(8,128)}) custom-call(f32[4,128,128]{2,1,0:T(8,128)} %z.3, f32[4,128,128]{2,1,0:T(8,128)} %v.3, f32[4,128,128]{2,1,0:T(8,128)} %h.3, s32[128,128]{1,0:T(8,128)} %ls.3, f32[128,128]{1,0:T(8,128)} %vi.3, f32[2,128,128]{2,1,0:T(8,128)} %w.3, ...), custom_call_target="tpu_custom_call" | custom-call | tf_op jit(solution)/shard_map/step/pallas_call | solution.py:484

commit v3 on v2

--- a/solution.py
+++ b/solution.py
@@ -27,113 +27,17 @@
 BLOCK = STEP * EXT
 
 
-def exchange_kernel(
-    z, v, h, ls, vi, w, xw, xe, nh, sh, own, sea_i, sb, nb, load_sem, send_sem, recv_sem
-):
-    ox, oy = lax.axis_index("ox"), lax.axis_index("oy")
-    nx, ny = lax.axis_size("ox"), lax.axis_size("oy")
-    east, west = lax.rem(ox + 1, nx), lax.rem(ox + nx - 1, nx)
-    north, south = lax.rem(oy + 1, ny), lax.rem(oy + ny - 1, ny)
-    peers = (
-        (east, oy), (west, oy), (ox, north), (ox, south),
-        (east, north), (east, south), (west, north), (west, south),
-    )
-    barrier = pltpu.get_barrier_semaphore()
-    for peer in peers:
-        pl.semaphore_signal(barrier, inc=1, device_id=peer, device_id_type=MESH)
-    loads = [
-        pltpu.make_async_copy(src, dst, load_sem.at[k])
-        for k, (src, dst) in enumerate((
-            (z, own.at[0:4]), (v, own.at[4:8]), (h, own.at[8:12]), (ls, sea_i),
-            (vi, own.at[VISC]), (w, own.at[WIND : WIND + 2]),
-        ))
-    ]
-    for copy in loads:
-        copy.start()
-    for copy in loads:
-        copy.wait()
-
-    lane = lax.broadcasted_iota(jnp.int32, (8, N), 1)
-    low = lax.rem(lane, 16) < 8
-
-    def pack(k, carry):
-        rows = pl.ds(pl.multiple_of(8 * k, 8), 8)
-        own[SEA, rows, :] = sea_i[rows, :].astype(F32)
-        halves = []
-        for m in range(2):
-            packed = own[8 * m, rows, :]
-            for j in range(1, 8):
-                moved = pltpu.roll(own[8 * m + j, rows, :], 16 * j, 1)
-                packed = jnp.where((lane >= 16 * j - 8) & (lane < 16 * j + 8), moved, packed)
-            halves.append(packed)
-        sb[rows, :] = jnp.where(low, halves[0], pltpu.roll(halves[1], 8, 1))
-        nb[rows, :] = jnp.where(low, pltpu.roll(halves[1], N - 8, 1), halves[0])
-        return carry
-
-    lax.fori_loop(0, N // 8, pack, 0)
-    pl.semaphore_wait(barrier, 8)
-
-    first, last = pl.ds(0, 8), pl.ds(N - 8, 8)
-    moves = (
-        (own.at[:, last], xw, (east, oy)),
-        (own.at[:, first], xe, (west, oy)),
-        (nb, sh.at[8 : 8 + N], (ox, north)),
-        (sb, nh.at[8 : 8 + N], (ox, south)),
-        (nb.at[last], sh.at[0:8], (east, north)),
-        (sb.at[last], nh.at[0:8], (east, south)),
-        (nb.at[first], sh.at[N + 8 : EXT], (west, north)),
-        (sb.at[first], nh.at[N + 8 : EXT], (west, south)),
-    )
-    sends = [
-        pltpu.make_async_remote_copy(
-            src_ref=src, dst_ref=dst, send_sem=send_sem.at[k], recv_sem=recv_sem.at[k],
-            device_id=peer, device_id_type=MESH,
-        )
-        for k, (src, dst, peer) in enumerate(moves)
-    ]
-    for copy in reversed(sends):
-        copy.start()
-    for copy in sends:
-        copy.wait()
-
-
-def exchange(z, v, h, ls, vi, w):
-    any_spec = pl.BlockSpec(memory_space=pl.ANY)
-    strip = jax.ShapeDtypeStruct((FIELDS, 8, N), F32)
-    side = jax.ShapeDtypeStruct((EXT, N), F32)
-    return pl.pallas_call(
-        exchange_kernel,
-        out_shape=(strip, strip, side, side),
-        in_specs=[any_spec] * 6,
-        out_specs=[any_spec] * 4,
-        scratch_shapes=[
-            pltpu.VMEM((FIELDS, N, N), F32),
-            pltpu.VMEM((N, N), jnp.int32),
-            pltpu.VMEM((N, N), F32),
-            pltpu.VMEM((N, N), F32),
-            pltpu.SemaphoreType.DMA((6,)),
-            pltpu.SemaphoreType.DMA((8,)),
-            pltpu.SemaphoreType.DMA((8,)),
-        ],
-        compiler_params=pltpu.CompilerParams(collective_id=0, has_side_effects=True),
-        name="exchange",
-    )(z, v, h, ls, vi, w)
-
-
 def build_weights(conv1, conv2, conv3, first_w, second_w, last_w, rows24):
     lane = lax.broadcasted_iota(jnp.int32, (8, N), 1)
     right = lane >= HID
     row = lax.broadcasted_iota(jnp.int32, (8, N), 0)
 
-    scale = lax.broadcasted_iota(jnp.int32, (16, 4), 0) == lax.broadcasted_iota(jnp.int32, (16, 4), 1)
-    scale = jnp.where(scale, 0.5, 0.0).astype(BF16)
     nt = (((1,), (1,)), ((), ()))
     taps = {}
     for a in range(3):
         for b in range(3):
-            one = conv1[a, b]
-            both = jnp.concatenate([one, one], axis=0)
-            taps[a, b] = lax.dot_general(scale, both, nt, preferred_element_type=F32)
+            one = conv1[a, b].astype(F32) * 0.5
+            taps[a, b] = jnp.concatenate([one, one], axis=1)
     for b in range(3):
         for c in range(4):
             vecs = [jnp.broadcast_to(taps[a, b][c : c + 1], (8, N)) for a in range(3)]
@@ -172,24 +76,33 @@
             for m in range(4):
                 a = m - i + 2
                 if 0 <= a < 3:
-                    rows24[8 * b + place : 8 * b + place + 1, HID * m : HID * m + HID] = conv3[a, b].astype(F32)
+                    rows24[8 * b + place : 8 * b + place + 1, HID * m : HID * m + HID] = conv3[a, 0, b : b + 1].astype(F32)
     last_w[...] = rows24[...].astype(BF16)
 
 
 def step_kernel(
-    z, v, h, ls, vi, w, xw, xe, nh, sh, grav, conv1, bias1, conv2, bias2, conv3,
+    z, v, h, ls, vi, w, grav, conv1, bias1, conv2, bias2, conv3,
     z_out, v_out, h_out, visc_out,
     f0, f1, sea_i, ns, p0, p1, t0, t1, zo, vo, fs, ft, h1, d0, d1, rs, re, nat,
-    first_w, second_w, last_w, rows24, load_sem, store_sem,
+    first_w, second_w, last_w, rows24, sb, nb, xw, xe, load_sem, store_sem, send_sem, recv_sem,
 ):
-    oy, ny = lax.axis_index("oy"), lax.axis_size("oy")
+    ox, oy = lax.axis_index("ox"), lax.axis_index("oy")
+    nx, ny = lax.axis_size("ox"), lax.axis_size("oy")
+    east, west = lax.rem(ox + 1, nx), lax.rem(ox + nx - 1, nx)
+    above, below = lax.rem(oy + 1, ny), lax.rem(oy + ny - 1, ny)
+    peers = (
+        (east, oy), (west, oy), (ox, above), (ox, below),
+        (east, above), (east, below), (west, above), (west, below),
+    )
+    barrier = pltpu.get_barrier_semaphore()
+    for peer in peers:
+        pl.semaphore_signal(barrier, inc=1, device_id=peer, device_id_type=MESH)
     mid = pl.ds(16, N)
     loads = [
         pltpu.make_async_copy(src, dst, load_sem.at[k])
         for k, (src, dst) in enumerate((
             (z, f0.at[0:4, mid]), (v, f0.at[4:8, mid]), (h, f0.at[8:12, mid]), (ls, sea_i),
             (vi, f0.at[VISC, mid]), (w, f0.at[WIND : WIND + 2, mid]),
-            (xw, f0.at[:, 8:16]), (xe, f0.at[:, N + 16 : N + 24]), (nh, ns.at[0]), (sh, ns.at[1]),
         ))
     ]
     for copy in loads:
@@ -206,7 +119,6 @@
     for c in range(4):
         for t in range(2):
             fs[c, t, EXT + 8 : TALL, :] = jnp.zeros((TALL - EXT - 8, N), F32)
-    build_weights(conv1, conv2, conv3, first_w, second_w, last_w, rows24)
 
     has_north = (oy < ny - 1).astype(F32)
     has_south = (oy > 0).astype(F32)
@@ -216,6 +128,56 @@
 
     def lanes(rows):
         return lax.broadcasted_iota(jnp.int32, (rows, N), 1)
+
+    f0[SEA, mid, :] = sea_i[...].astype(F32)
+    for k in range(8):
+        f0[k, mid, :] = f0[k, mid, :] * f0[SEA, mid, :]
+
+    def pack(k, carry):
+        rows = pl.ds(pl.multiple_of(PACK * k, 8), PACK)
+        src = pl.ds(pl.multiple_of(PACK * k + 16, 8), PACK)
+        lane = lanes(PACK)
+        low = lax.rem(lane, 16) < 8
+        halves = []
+        for m in range(2):
+            packed = f0[8 * m, src, :]
+            for j in range(1, 8):
+                moved = pltpu.roll(f0[8 * m + j, src, :], 16 * j, 1)
+                packed = jnp.where((lane >= 16 * j - 8) & (lane < 16 * j + 8), moved, packed)
+            halves.append(packed)
+        sb[rows, :] = jnp.where(low, halves[0], pltpu.roll(halves[1], 8, 1))
+        nb[rows, :] = jnp.where(low, pltpu.roll(halves[1], N - 8, 1), halves[0])
+        return carry
+
+    lax.fori_loop(0, N // PACK, pack, 0)
+    pl.semaphore_wait(barrier, 8)
+
+    first, last = pl.ds(0, 8), pl.ds(N - 8, 8)
+    moves = (
+        (nb, ns.at[1, 8 : 8 + N], (ox, above)),
+        (sb, ns.at[0, 8 : 8 + N], (ox, below)),
+        (f0.at[:, N + 8 : N + 16], xw, (east, oy)),
+        (f0.at[:, 16:24], xe, (west, oy)),
+        (nb.at[last], ns.at[1, 0:8], (east, above)),
+        (sb.at[last], ns.at[0, 0:8], (east, below)),
+        (nb.at[first], ns.at[1, N + 8 : EXT], (west, above)),
+        (sb.at[first], ns.at[0, N + 8 : EXT], (west, below)),
+    )
+    sends = [
+        pltpu.make_async_remote_copy(
+            src_ref=src, dst_ref=dst, send_sem=send_sem.at[k], recv_sem=recv_sem.at[k],
+            device_id=peer, device_id_type=MESH,
+        )
+        for k, (src, dst, peer) in enumerate(moves)
+    ]
+    for copy in reversed(sends):
+        copy.start()
+    build_weights(conv1, conv2, conv3, first_w, second_w, last_w, rows24)
+    for copy in sends:
+        copy.wait()
+    for k in range(FIELDS):
+        f0[k, 8:16, :] = xw[k]
+        f0[k, N + 16 : N + 24, :] = xe[k]
 
     def north(a, b):
         last_lane = lanes(a.shape[0]) == N - 1
@@ -226,8 +188,6 @@
         first_lane = lanes(a.shape[0]) == 0
         a, b = pltpu.roll(a, 1, 1), pltpu.roll(b, 1, 1)
         return jnp.where(first_lane, b, a), jnp.where(first_lane, a, b)
-
-    f0[SEA, mid, :] = sea_i[...].astype(F32)
 
     def spread(k, carry):
         size = SPREAD
@@ -246,15 +206,13 @@
             pack, j = packs[field // 8], field % 8
             return pltpu.roll(pack, N - 16 * j, 1) if j else pack
 
-        sea0 = f0[SEA, rows, :]
         sea1 = side(SEA) * inside
         f1[SEA, rows, :] = sea1
         f1[VISC, rows, :] = side(VISC) * inside
         for field in (8, 9, 10, 11, WIND, WIND + 1):
             f1[field, rows, :] = side(field)
         for field in range(8):
-            f1[field, rows, :] = side(field) * sea1
-            f0[field, rows, :] = f0[field, rows, :] * sea0
+            f1[field, rows, :] = side(field) * inside
         return carry
 
     lax.fori_loop(0, EXT // SPREAD, spread, 0)
@@ -474,17 +432,17 @@
     copy_v.wait()
 
 
-SPREAD, CONT, MOM = 48, 24, 16
-
-
-def step(fields, strips, grav, conv1, bias1, conv2, bias2, conv3):
+PACK, SPREAD, CONT, MOM = 32, 48, 24, 16
+
+
+def step(fields, grav, conv1, bias1, conv2, bias2, conv3):
     any_spec = pl.BlockSpec(memory_space=pl.ANY)
     vmem = pl.BlockSpec(memory_space=pltpu.VMEM)
     whole = jax.ShapeDtypeStruct((LAYERS, N, N), F32)
     return pl.pallas_call(
         step_kernel,
         out_shape=(whole, whole, whole, jax.ShapeDtypeStruct((N, N), F32)),
-        in_specs=[any_spec] * 10 + [pl.BlockSpec(memory_space=pltpu.SMEM)] + [vmem] * 5,
+        in_specs=[any_spec] * 6 + [pl.BlockSpec(memory_space=pltpu.SMEM)] + [vmem] * 5,
         out_specs=[any_spec] * 3 + [vmem],
         scratch_shapes=[
             pltpu.VMEM((FIELDS, PAD, N), F32),
@@ -509,18 +467,27 @@
             pltpu.VMEM((18 * HID, 4 * HID), BF16),
             pltpu.VMEM((32, 2 * N), BF16),
             pltpu.VMEM((32, 2 * N), F32),
-            pltpu.SemaphoreType.DMA((10,)),
+            pltpu.VMEM((N, N), F32),
+            pltpu.VMEM((N, N), F32),
+            pltpu.VMEM((FIELDS, 8, N), F32),
+            pltpu.VMEM((FIELDS, 8, N), F32),
+            pltpu.SemaphoreType.DMA((6,)),
             pltpu.SemaphoreType.DMA((3,)),
+            pltpu.SemaphoreType.DMA((8,)),
+            pltpu.SemaphoreType.DMA((8,)),
         ],
-        compiler_params=pltpu.CompilerParams(vmem_limit_bytes=56 * 2**20),
+        compiler_params=pltpu.CompilerParams(
+            collective_id=0, has_side_effects=True, vmem_limit_bytes=56 * 2**20
+        ),
         name="step",
-    )(*fields, *strips, grav, conv1, bias1, conv2, bias2, conv3)
+    )(*fields, grav, conv1, bias1, conv2, bias2, conv3)
 
 
 def local(z, v, h, ls, vi, w, grav, conv1, bias1, conv2, bias2, conv3):
     fields = (z, v, h, ls, vi, w)
-    strips = exchange(*fields)
-    return step(fields, strips, grav, conv1, bias1, conv2, bias2, conv3)
+    conv1 = jnp.transpose(conv1, (0, 1, 3, 2))
+    conv3 = jnp.transpose(conv3, (0, 2, 1, 3))
+    return step(fields, grav, conv1, bias1, conv2, bias2, conv3)
 
 
 def solution(mesh):

time: 32.6 us -> 34.5 us (1.058)
  the two profiles are of different devices: /device:TPU:25 before, /device:TPU:0 now
where the time goes in v3:
time: 34.5 us; the launch traced here: 34.3 us
  Pallas kernels  29.4 us (85%)
  local copies, waits for them, and re-layouts  4.25 us (12%)
  between operations  0.66 us (2%)
    pallas_call x1, Pallas kernels, step(): pl.pallas_call(step_kernel, out_shape=(whole, whole, whole, jax.ShapeDtyp...  29.4 us
    unnamed x10, local copies, waits for them, and re-layouts  4.25 us

profile of v3, /device:TPU:0, one launch (start us, length us, event | category | flops | bytes accessed | tf_op | source)
XLA Modules:
  0.0 34.3 jit_solution(13759318822035291207)
XLA Ops:
  0.6 29.4 %step.1 = (f32[4,128,128]{2,1,0:T(8,128)}, f32[4,128,128]{2,1,0:T(8,128)}, f32[4,128,128]{2,1,0:T(8,128)}, f32[128,128]{1,0:T(8,128)}) custom-call(f32[4,128,128]{2,1,0:T(8,128)} %z.1, f32[4,128,128]{2,1,0:T(8,128)} %v.1, f32[4,128,128]{2,1,0:T(8,128)} %h.1, s32[128,128]{1,0:T(8,128)} %ls.1, f32[128,128]{1,0:T(8,128)} %vi.1, f32[2,128,128]{2,1,0:T(8,128)} %w.1, ...), custom_call_target="tpu_custom_call" | custom-call | tf_op jit(solution)/shard_map/step/pallas_call | solution.py:442
  30.0 0.0 copy-start.1
  30.0 1.7 %copy.20 = f32[4,128,128]{2,1,0:T(8,128)} copy(f32[4,128,128]{2,1,0:T(8,128)} %get-tuple-element.8) | data formatting | bytes 524288
  31.7 0.0 copy-done.1
  31.7 0.0 copy-start
  31.7 0.7 %copy.21 = f32[4,128,128]{2,1,0:T(8,128)} copy(f32[4,128,128]{2,1,0:T(8,128)S(1)} %copy-done.1) | data formatting | bytes 524288
  32.4 0.3 copy-done
  32.8 0.0 copy-start.2
  32.8 0.7 %copy.22 = f32[4,128,128]{2,1,0:T(8,128)} copy(f32[4,128,128]{2,1,0:T(8,128)S(1)} %copy-done) | data formatting | bytes 524288
  33.5 0.2 copy-done.2
  33.6 0.6 %copy.23 = f32[128,128]{1,0:T(8,128)} copy(f32[128,128]{1,0:T(8,128)S(1)} %copy-done.2) | data formatting | bytes 131072
Async XLA Ops:
  30.0 1.7 %copy-start.1 = (f32[4,128,128]{2,1,0:T(8,128)S(1)}, f32[4,128,128]{2,1,0:T(8,128)}, u32[]{:S(2)}) copy-start(f32[4,128,128]{2,1,0:T(8,128)} %get-tuple-element.9) | copy-start | bytes 786436
  31.7 1.0 %copy-start = (f32[4,128,128]{2,1,0:T(8,128)S(1)}, f32[4,128,128]{2,1,0:T(8,128)}, u32[]{:S(2)}) copy-start(f32[4,128,128]{2,1,0:T(8,128)} %get-tuple-element.10) | copy-start | bytes 786436
  32.8 0.9 %copy-start.2 = (f32[128,128]{1,0:T(8,128)S(1)}, f32[128,128]{1,0:T(8,128)}, u32[]{:S(2)}) copy-start(f32[128,128]{1,0:T(8,128)} %get-tuple-element.11) | copy-start | bytes 196612

commit v4 on v2

v4 whole, which is shorter than its diff:
```python
import jax
import jax.numpy as jnp
from jax import lax
from jax.experimental import pallas as pl
from jax.experimental.pallas import tpu as pltpu
from jax.sharding import PartitionSpec as P

MESH = pl.DeviceIdType.MESH
F32 = jnp.float32
BF16 = jnp.bfloat16

DT = 0.05
REST = 1.4
DRAG = 0.5
LAYERS = 4
N = 128
HID = 64
FIELDS = 16
SEA, VISC, WIND = 12, 13, 14
EXT = N + 16
PAD = N + 32
TALL = N + 40
PAIRS = 72
GROUPS = 33
STEP = 3
TILES = EXT // 16
BLOCK = STEP * EXT


HBM = pltpu.HBM
EDGE = 32


def lanes(rows):
    return lax.broadcasted_iota(jnp.int32, (rows, N), 1)


def near(x):
    return pltpu.roll(x, N - 1, 1), pltpu.roll(x, 1, 1)


def shifted(start, size):
    aligned = start if isinstance(start, int) else pl.multiple_of(start, 8)
    return pl.ds(aligned, size), pl.ds(start + 1, size), pl.ds(start - 1, size)


def continuity(f, press, depth, grav, start, size):
    rows, up, down = shifted(start, size)
    sea = f[SEA, rows, :]
    anomaly = []
    for l in range(LAYERS):
        thick = f[8 + l, rows, :]
        fn, fs = near(f[4 + l, rows, :] * thick)
        fe = f[l, up, :] * f[8 + l, up, :]
        fw = f[l, down, :] * f[8 + l, down, :]
        diverge = (fe - fw) * 0.5 + (fn - fs) * 0.5
        new = thick - DT * sea * diverge
        depth[l, rows, :] = new
        anomaly.append(new - REST)
    faces = [anomaly[3]]
    for l in (2, 1, 0):
        faces.insert(0, faces[0] + anomaly[l])
    total = grav[0] * faces[0]
    press[0, rows, :] = total
    for l in range(1, LAYERS):
        total = total + grav[l] * faces[l]
        press[l, rows, :] = total


def coefficients(visc, up, down):
    return [0.5 * (visc + other) for other in (up, down, *near(visc))]


def viscous(coef, centre, up, down):
    total = None
    for c, q in zip(coef, (up, down, *near(centre))):
        term = c * (q - centre)
        total = term if total is None else total + term
    return total


def coriolis_of(lat, ny):
    return 0.3 + 1.4 * (lat.astype(F32) + 0.5) / (N * ny)


def momentum(f, press, depth, zo, vo, feature_refs, coriolis, start, size):
    rows, up, down = shifted(start, size)
    sea = f[SEA, rows, :]
    coef = coefficients(f[VISC, rows, :], f[VISC, up, :], f[VISC, down, :])
    kinetic = column = None
    for l in range(LAYERS):
        zc, vc = f[l, rows, :], f[4 + l, rows, :]
        pn, ps = near(press[l, rows, :])
        gx = (press[l, up, :] - press[l, down, :]) * 0.5
        gy = (pn - ps) * 0.5
        thick = depth[l, rows, :]
        fz = coriolis * vc - gx + viscous(coef, zc, f[l, up, :], f[l, down, :])
        fv = -coriolis * zc - gy + viscous(coef, vc, f[4 + l, up, :], f[4 + l, down, :])
        if l == 0:
            fz = fz + f[WIND, rows, :] / thick
            fv = fv + f[WIND + 1, rows, :] / thick
        if l == LAYERS - 1:
            fz = fz - DRAG * zc
            fv = fv - DRAG * vc
        z_new = sea * (zc + DT * fz)
        v_new = sea * (vc + DT * fv)
        zo[l, rows, :] = z_new
        vo[l, rows, :] = v_new
        part = thick * (z_new * z_new + v_new * v_new)
        kinetic = part if l == 0 else kinetic + part
        column = thick if l == 0 else column + thick
        if l == 0:
            feature_refs[0][0, rows, :] = z_new
            feature_refs[0][1, rows, :] = v_new
            feature_refs[0][2, rows, :] = sea * (thick - REST)
    feature_refs[0][3, rows, :] = sea * (0.5 * kinetic / column)


def own_pack(read, lane):
    packed = None
    for l in range(4):
        field = read(l)
        for at, shift in ((32 * l + 8, 32 * l + 8), (32 * l + 16, 32 * l + 16 + 8)):
            moved = pltpu.roll(field, shift % N, 1)
            packed = moved if packed is None else jnp.where((lane >= at) & (lane < at + 8), moved, packed)
    return packed


def exchange_kernel(
    z, v, h, ls, vi, w, grav_in, conv1, conv2, conv3, bias1, bias2,
    f0, p0, t0, zo, vo, fs, ft, own, ns, xw, xe, first_w, second_w, last_w, consts,
    sea_i, sb, nb, rows24, c1, c2, c3, grav, s1, s2, load_sem, send_sem, recv_sem,
):
    ox, oy = lax.axis_index("ox"), lax.axis_index("oy")
    nx, ny = lax.axis_size("ox"), lax.axis_size("oy")
    east, west = lax.rem(ox + 1, nx), lax.rem(ox + nx - 1, nx)
    above, below = lax.rem(oy + 1, ny), lax.rem(oy + ny - 1, ny)
    peers = (
        (east, oy), (west, oy), (ox, above), (ox, below),
        (east, above), (east, below), (west, above), (west, below),
    )
    barrier = pltpu.get_barrier_semaphore()
    for peer in peers:
        pl.semaphore_signal(barrier, inc=1, device_id=peer, device_id_type=MESH)
    mid = pl.ds(16, N)
    loads = [
        pltpu.make_async_copy(src, dst, load_sem.at[k])
        for k, (src, dst) in enumerate((
            (ls, sea_i), (z, f0.at[0:4, mid]), (v, f0.at[4:8, mid]), (h, f0.at[8:12, mid]),
            (vi, f0.at[VISC, mid]), (w, f0.at[WIND : WIND + 2, mid]),
            (conv1, c1), (conv2, c2), (conv3, c3), (grav_in, grav), (bias1, s1), (bias2, s2),
        ))
    ]
    for copy in loads:
        copy.start()
    ones = jnp.ones((8, N), F32)
    for rows in (pl.ds(8, 8), pl.ds(N + 16, 8)):
        for k in range(FIELDS):
            f0[k, rows, :] = ones
        for k in range(LAYERS):
            p0[k, rows, :] = ones
    for copy in loads[:6]:
        copy.wait()

    def pack(k, carry):
        src = pl.ds(pl.multiple_of(PACK * k + 16, 8), PACK)
        rows = pl.ds(pl.multiple_of(PACK * k, 8), PACK)
        lane = lanes(PACK)
        sea = sea_i[rows, :].astype(F32)
        f0[SEA, src, :] = sea
        to_south = to_north = None
        for a in range(4):
            for l in range(4):
                field = sea if 4 * a + l == SEA else f0[4 * a + l, src, :]
                if a < 2:
                    field = field * sea
                    f0[4 * a + l, src, :] = field
                at = 32 * l + 8 * a
                moved = pltpu.roll(field, at, 1) if at else field
                if to_south is None:
                    to_south = to_north = moved
                else:
                    to_south = jnp.where((lane >= at) & (lane < at + 8), moved, to_south)
                    to_north = jnp.where((lane >= at - 8) & (lane < at), moved, to_north)
        sb[rows, :] = to_south
        nb[rows, :] = to_north
        return carry

    lax.fori_loop(0, N // PACK, pack, 0)
    pl.semaphore_wait(barrier, 8)

    first, last = pl.ds(0, 8), pl.ds(N - 8, 8)
    moves = (
        (nb, ns.at[1, 8 : 8 + N], (ox, above)),
        (sb, ns.at[0, 8 : 8 + N], (ox, below)),
        (f0.at[:, N + 8 : N + 16], xw, (east, oy)),
        (f0.at[:, 16:24], xe, (west, oy)),
        (nb.at[last], ns.at[1, 0:8], (east, above)),
        (sb.at[last], ns.at[0, 0:8], (east, below)),
        (nb.at[first], ns.at[1, N + 8 : EXT], (west, above)),
        (sb.at[first], ns.at[0, N + 8 : EXT], (west, below)),
    )
    sends = [
        pltpu.make_async_remote_copy(
            src_ref=src, dst_ref=dst, send_sem=send_sem.at[k], recv_sem=recv_sem.at[k],
            device_id=peer, device_id_type=MESH,
        )
        for k, (src, dst, peer) in enumerate(moves)
    ]
    for copy in reversed(sends):
        copy.start()

    for copy in loads[6:]:
        copy.wait()
    build_weights(c1, c2, c3, first_w, second_w, last_w, rows24)
    for l in range(LAYERS):
        consts[l : l + 1, :] = jnp.full((1, N), grav[l], F32)
    for k, bias in enumerate((s1, s2)):
        half = bias[...].reshape(1, HID) * 0.5
        consts[4 + k : 5 + k, :] = jnp.concatenate([half, half], axis=1)

    def inner_continuity(k, carry):
        continuity(f0, p0, t0, grav, CONT * k + 16, CONT)
        return carry

    lax.fori_loop(0, N // CONT, inner_continuity, 0)

    def inner_momentum(k, carry):
        coriolis = coriolis_of(oy * N + lanes(MOM), ny)
        momentum(f0, p0, t0, zo, vo, (fs,), coriolis, MOM * k + 16, MOM)
        return carry

    lax.fori_loop(0, N // MOM, inner_momentum, 0)

    def inner_pack(k, carry):
        src = pl.ds(pl.multiple_of(OWN * k + 16, 8), OWN)
        rows = pl.ds(pl.multiple_of(OWN * k, 8), OWN)
        for a in range(4):
            own[a, rows, :] = own_pack(lambda l: f0[4 * a + l, src, :], lanes(OWN))
        return carry

    lax.fori_loop(0, N // OWN, inner_pack, 0)

    def inner_turn(k, carry):
        rows = pl.ds(pl.multiple_of(16 * k + 24, 8), 32)
        ft[k] = fs[:, rows, :].reshape(N, N).T
        return carry

    lax.fori_loop(0, 6, inner_turn, 0)
    for copy in sends:
        copy.wait()


def exchange(fields, grav, conv1, conv2, conv3, bias1, bias2):
    hbm = pl.BlockSpec(memory_space=HBM)
    vmem = pl.BlockSpec(memory_space=pltpu.VMEM)

    def array(*shape, dtype=F32):
        return jax.ShapeDtypeStruct(shape, dtype)

    return pl.pallas_call(
        exchange_kernel,
        out_shape=(
            array(FIELDS, PAD, N), array(LAYERS, PAD, N), array(LAYERS, PAD, N),
            array(LAYERS, PAD, N), array(LAYERS, PAD, N), array(4, PAD, N),
            array(6, N, N), array(4, N, N), array(2, EXT, N),
            array(FIELDS, 8, N), array(FIELDS, 8, N),
            array(3 * N, 16 * HID, dtype=BF16), array(18 * HID, 4 * HID, dtype=BF16),
            array(32, 2 * N, dtype=BF16), array(8, N),
        ),
        in_specs=[hbm] * 12,
        out_specs=(vmem,) * 15,
        scratch_shapes=[
            pltpu.VMEM((N, N), jnp.int32),
            pltpu.VMEM((N, N), F32),
            pltpu.VMEM((N, N), F32),
            pltpu.VMEM((32, 2 * N), F32),
            pltpu.VMEM(conv1.shape, BF16),
            pltpu.VMEM(conv2.shape, BF16),
            pltpu.VMEM(conv3.shape, BF16),
            pltpu.SMEM((LAYERS,), F32),
            pltpu.VMEM((HID,), F32),
            pltpu.VMEM((HID,), F32),
            pltpu.SemaphoreType.DMA((12,)),
            pltpu.SemaphoreType.DMA((8,)),
            pltpu.SemaphoreType.DMA((8,)),
        ],
        compiler_params=pltpu.CompilerParams(
            collective_id=0, has_side_effects=True, vmem_limit_bytes=16 * 2**20
        ),
        name="exchange",
    )(*fields, grav, conv1, conv2, conv3, bias1, bias2)


def build_weights(conv1, conv2, conv3, first_w, second_w, last_w, rows24):
    lane = lax.broadcasted_iota(jnp.int32, (8, N), 1)
    right = lane >= HID
    row = lax.broadcasted_iota(jnp.int32, (8, N), 0)

    nt = (((1,), (1,)), ((), ()))
    taps = {}
    for a in range(3):
        for b in range(3):
            one = conv1[a, b].astype(F32) * 0.5
            taps[a, b] = jnp.concatenate([one, one], axis=1)
    for b in range(3):
        for c in range(4):
            vecs = [jnp.broadcast_to(taps[a, b][c : c + 1], (8, N)) for a in range(3)]
            for jp in range(8):
                parts = []
                for i in range(4):
                    gap = row + 8 * i - 2 * jp - jnp.where(right, 1, 0) - 4
                    val = jnp.zeros((8, N), F32)
                    for a in range(3):
                        val = jnp.where(gap == a, vecs[a], val)
                    parts.append(val)
                start = 128 * b + 32 * c
                first_w[start : start + 32, N * jp : N * jp + N] = jnp.concatenate(parts, 0).astype(BF16)

    eye = lax.broadcasted_iota(jnp.int32, (HID, HID), 0) == lax.broadcasted_iota(jnp.int32, (HID, HID), 1)
    eye = jnp.where(eye, 0.5, 0.0).astype(BF16)
    side = lax.broadcasted_iota(jnp.int32, (HID, N), 1) >= HID
    for b in range(3):
        turned = []
        for a in range(3):
            one = conv2[a, b]
            both = jnp.concatenate([one, one], axis=0)
            turned.append(lax.dot_general(eye, both, nt, preferred_element_type=F32))
        zero = jnp.zeros((HID, N), F32)
        for m in range(6):
            for jp in range(2):
                tap = m - 2 * jp
                left = turned[tap] if 0 <= tap < 3 else zero
                other = turned[tap - 1] if 0 <= tap - 1 < 3 else zero
                start = (6 * b + m) * HID
                second_w[start : start + HID, N * jp : N * jp + N] = jnp.where(side, other, left).astype(BF16)

    rows24[...] = jnp.zeros((32, 2 * N), F32)
    for b in range(3):
        for place, i in ((0, 3), (1, 4), (2, 5), (5, 0), (6, 1), (7, 2)):
            for m in range(4):
                a = m - i + 2
                if 0 <= a < 3:
                    rows24[8 * b + place : 8 * b + place + 1, HID * m : HID * m + HID] = conv3[a, 0, b : b + 1].astype(F32)
    last_w[...] = rows24[...].astype(BF16)


def step_kernel(
    f0, p0, t0, zo, vo, fs0, ft0, own, ns, xw, xe, first_w, second_w, last_w, consts,
    z_out, v_out, h_out, visc_out,
    fe, pe, te, ze, ve, fse, q, pq, hq, zq, vq, fsq, fs, ft, zm, vm, hm, h1, d0, d1, rs, re, nat,
    store_sem,
):
    oy, ny = lax.axis_index("oy"), lax.axis_size("oy")
    has_north = (oy < ny - 1).astype(F32)
    has_south = (oy > 0).astype(F32)
    ones = jnp.ones((8, N), F32)
    grav = [consts[l : l + 1, :] for l in range(LAYERS)]

    for e, (rows, src) in enumerate((((8, xw), (16, 16)), ((0, N), (16, xe)))):
        (halo_at, halo), (own_at, own_from) = (rows, src) if e == 0 else (src, rows)
        pad = 0 if e == 0 else 24
        for k in range(FIELDS):
            fe[e, k, halo_at : halo_at + 8, :] = halo[k]
            fe[e, k, own_at : own_at + 16, :] = f0[k, own_from : own_from + 16, :]
            fe[e, k, pad : pad + 8, :] = ones
        inner_at, inner_from = (24, 24) if e == 0 else (0, N)
        for k in range(LAYERS):
            pe[e, k, pad : pad + 8, :] = ones
            pe[e, k, inner_at : inner_at + 8, :] = p0[k, inner_from : inner_from + 8, :]
    for e in range(2):
        continuity(fe.at[e], pe.at[e], te.at[e], grav, 8, 16)
    for e in range(2):
        coriolis = coriolis_of(oy * N + lanes(16), ny)
        momentum(fe.at[e], pe.at[e], te.at[e], ze.at[e], ve.at[e], (fse.at[e],), coriolis, 8, 16)

    for k in range(7):
        q[k, 0:8, :] = ones
        q[k, PAD - 8 : PAD, :] = ones
    pq[0:8, :] = ones
    pq[PAD - 8 : PAD, :] = ones
    for c in range(4):
        fs[c, EXT + 8 : TALL, :] = jnp.zeros((TALL - EXT - 8, N), F32)
        fsq[c, EXT + 8 : TALL, :] = jnp.zeros((TALL - EXT - 8, N), F32)

    def spread(start, size, groups):
        lane = lanes(size)
        part = lax.rem(lane, 32)
        seg = lane // 32
        inside = jnp.where(part < 8, has_south, jnp.where(part < 24, 1.0, has_north))
        rows = pl.ds(start + 8 if isinstance(start, int) else pl.multiple_of(start + 8, 8), size)
        src = pl.ds(start if isinstance(start, int) else pl.multiple_of(start, 8), size)
        from_north, from_south = ns[0, src, :], ns[1, src, :]
        full = []
        for a in range(4):
            high = pltpu.roll(from_north, (24 - 8 * a) % N, 1)
            low = pltpu.roll(from_south, (8 - 8 * a) % N, 1)
            full.append(jnp.where(part < 8, low, jnp.where(part < 24, groups(a), high)))
        q[0, rows, :] = full[0] * inside
        q[1, rows, :] = full[1] * inside
        q[2, rows, :] = full[2]
        for k, s in ((3, 0), (4, 1)):
            one = jnp.where(seg == s, full[3] * inside, 0.0)
            one = one + pltpu.roll(one, 32, 1)
            q[k, rows, :] = one + pltpu.roll(one, 64, 1)
        for k, s in ((5, 2), (6, 3)):
            q[k, rows, :] = jnp.where(seg == 0, pltpu.roll(full[3], N - 32 * s, 1), 0.0)

    for at, strip in ((0, xw), (N + 8, xe)):
        spread(at, 8, lambda a: own_pack(lambda l: strip[4 * a + l], lanes(8)))

    def spread_body(k, carry):
        rows = pl.ds(pl.multiple_of(SPREAD * k, 8), SPREAD)
        spread(SPREAD * k + 8, SPREAD, lambda a: own[a, rows, :])
        return carry

    lax.fori_loop(0, N // SPREAD, spread_body, 0)

    def packed_continuity(k, carry):
        size = QC
        lane = lanes(size)
        part, seg = lax.rem(lane, 32), lane // 32
        inside = jnp.where(part < 8, has_south, jnp.where(part < 24, 1.0, has_north))
        weight = jnp.where(seg == 0, grav[0], jnp.where(seg == 1, grav[1], jnp.where(seg == 2, grav[2], grav[3])))
        rows, up, down = shifted(size * k + 8, size)
        thick = q[2, rows, :]
        fn, fs_ = near(q[1, rows, :] * thick)
        fe_ = q[0, up, :] * q[2, up, :]
        fw_ = q[0, down, :] * q[2, down, :]
        diverge = (fe_ - fw_) * 0.5 + (fn - fs_) * 0.5
        new = thick - DT * q[3, rows, :] * diverge
        hq[rows, :] = new
        a = new - REST
        face = a
        for n in (1, 2, 3):
            face = face + jnp.where(seg < 4 - n, pltpu.roll(a, N - 32 * n, 1), 0.0)
        term = weight * face
        total = term
        for n in (1, 2, 3):
            total = total + jnp.where(seg >= n, pltpu.roll(term, 32 * n, 1), 0.0)
        pq[rows, :] = total * inside
        return carry

    lax.fori_loop(0, EXT // QC, packed_continuity, 0)

    def packed_momentum(k, carry):
        size = QM
        lane = lanes(size)
        part, seg = lax.rem(lane, 32), lane // 32
        coriolis = coriolis_of(oy * N + part + jnp.where(part < 16, -8, 104), ny)
        drag = jnp.where(seg == 3, DRAG, 0.0)
        rows, up, down = shifted(size * k + 8, size)
        zc, vc, sea = q[0, rows, :], q[1, rows, :], q[3, rows, :]
        coef = coefficients(q[4, rows, :], q[4, up, :], q[4, down, :])
        pn, ps = near(pq[rows, :])
        gx = (pq[up, :] - pq[down, :]) * 0.5
        gy = (pn - ps) * 0.5
        thick = hq[rows, :]
        fz = coriolis * vc - gx + viscous(coef, zc, q[0, up, :], q[0, down, :])
        fv = -coriolis * zc - gy + viscous(coef, vc, q[1, up, :], q[1, down, :])
        fz = fz + q[5, rows, :] / thick - drag * zc
        fv = fv + q[6, rows, :] / thick - drag * vc
        z_new = sea * (zc + DT * fz)
        v_new = sea * (vc + DT * fv)
        zq[rows, :] = z_new
        vq[rows, :] = v_new
        sums = []
        for one in (thick * (z_new * z_new + v_new * v_new), thick):
            one = one + pltpu.roll(one, 64, 1)
            sums.append(one + pltpu.roll(one, 32, 1))
        fsq[0, rows, :] = z_new
        fsq[1, rows, :] = v_new
        fsq[2, rows, :] = sea * (thick - REST)
        fsq[3, rows, :] = sea * (0.5 * sums[0] / sums[1])
        return carry

    lax.fori_loop(0, EXT // QM, packed_momentum, 0)

    for c in range(4):
        fs[c, 8:24, :] = fse[0, c, 8:24, :]
        fs[c, 24:40, :] = fs0[c, 24:40, :]
        fs[c, N - 8 : N + 8, :] = fs0[c, N - 8 : N + 8, :]
        fs[c, N + 8 : N + 24, :] = fse[1, c, 8:24, :]

    row = lax.broadcasted_iota(jnp.int32, (8, N), 0)
    for k in range(9):
        if 1 <= k <= 6:
            inner = ft0[k - 1]
        else:
            inner = fs[:, 16 * k + 8 : 16 * k + 40, :].reshape(N, N).T
        ends = fsq[:, 16 * k + 8 : 16 * k + 40, :].reshape(N, N).T
        low = jnp.where(row < 4, ends[8:16], inner[0:8])
        high = jnp.where(row >= 4, ends[16:24], inner[N - 8 : N])
        ft[k, 0:8, :] = ends[0:8]
        ft[k, 8:16, :] = low
        ft[k, 16:N, :] = inner[8 : N - 8]
        ft[k, N : N + 8, :] = high
        ft[k, N + 8 : N + 16, :] = ends[24:32]
        ft[k, N + 16 : N + 24, :] = ends[0:8]
        ft[k, N + 24 : N + 32, :] = low

    def merge(size, rows, packed_rows, sources):
        lane = lanes(size)
        for packed, out, read in sources:
            whole = packed[packed_rows, :]
            for l in range(LAYERS):
                low = pltpu.roll(whole, (N - 32 * l - 8) % N, 1)
                high = pltpu.roll(whole, (104 - 32 * l) % N, 1)
                out[l, rows, :] = jnp.where(lane < 4, low, jnp.where(lane >= N - 4, high, read(l)))

    order = lax.broadcasted_iota(jnp.int32, (EXT, 2 * N), 0)
    lat = 9 * lax.rem(order, 16) + order // 16
    keep = jnp.where(lat < N, 1.0, jnp.where(lat < N + 8, has_north, has_south)) > 0.5
    b1 = jnp.concatenate([consts[4:5, :]] * 2, axis=1)
    b2 = jnp.concatenate([consts[5:6, :]] * 2, axis=1)

    def activate(x, bias):
        x = x + bias
        return jnp.where(keep, x + x * jnp.tanh(x), 0.0)

    def first_layer(k, quarters):
        parts = []
        for b in range(3):
            pieces = []
            for t in range(TILES):
                for half in range(2):
                    pieces.append(ft[k, pl.ds(7 + t + b + 72 * half, 8, stride=9), :])
            parts.append(jnp.concatenate(pieces, axis=0).astype(BF16))
        left = jnp.concatenate(parts, axis=1)
        for quarter in range(quarters):
            out = jnp.dot(left, first_w[:, 256 * quarter : 256 * quarter + 256], preferred_element_type=F32)
            out = activate(out, b1)
            at = 4 * k + quarter
            for p in range(2):
                one = out[:, N * p : N * p + N]
                h1[at, p, 16 : 16 + EXT, :] = one.astype(BF16)
                h1[at, p, 0:16, :] = pltpu.roll(one[EXT - 16 : EXT], 1, 0).astype(BF16)
                h1[at, p, 16 + EXT : 32 + EXT, :] = pltpu.roll(one[0:16], 15, 0).astype(BF16)

    def first_body(k, carry):
        first_layer(k, 4)
        rows = pl.ds(pl.multiple_of(16 * k + 8, 8), 16)
        wide = pl.ds(pl.multiple_of(16 * k + 24, 8), 16)
        merge(16, rows, wide, (
            (zq, zm, lambda l: zo[l, wide, :]),
            (vq, vm, lambda l: vo[l, wide, :]),
            (hq, hm, lambda l: t0[l, wide, :]),
        ))
        return carry

    lax.fori_loop(0, 7, first_body, 0)
    for e, (at, inner) in enumerate(((0, 16), (N - 8, 8))):
        merge(8, pl.ds(at, 8), pl.ds(at + 16, 8), (
            (zq, zm, lambda l: ze[e, l, inner : inner + 8, :]),
            (vq, vm, lambda l: ve[e, l, inner : inner + 8, :]),
            (hq, hm, lambda l: te[e, l, inner : inner + 8, :]),
        ))
    first_layer(7, 4)
    first_layer(8, 2)
    stores = [
        pltpu.make_async_copy(src, dst, store_sem.at[k])
        for k, (src, dst) in enumerate(((zm, z_out), (vm, v_out), (hm, h_out)))
    ]
    for copy in stores:
        copy.start()

    def second_matmul(k, ref):
        g = k * STEP
        parts = []
        for b in range(3):
            for d in range(3):
                block = h1[pl.ds(g + d // 2, STEP), d % 2, 16 * b : 16 * b + EXT, :]
                parts.append(block.reshape(BLOCK, N))
        left = jnp.concatenate(parts, axis=1)
        ref[...] = jnp.dot(left, second_w[...], preferred_element_type=F32)

    def finish(k, ref):
        for i in range(STEP):
            one = activate(ref[i * EXT : (i + 1) * EXT], b2).astype(BF16)
            sums = lax.dot_general(
                last_w[...], one, (((1,), (1,)), ((), ())), preferred_element_type=F32
            )
            rs[k * STEP + i] = sums[0:24, 0:N]
            re[k * STEP + i, :, 0:16] = sums[0:24, N:EXT]

    second_matmul(0, d0)

    def second_layer(k, carry):
        second_matmul(2 * k + 1, d1)
        finish(2 * k, d0)
        second_matmul(2 * k + 2, d0)
        finish(2 * k + 1, d1)
        return carry

    lax.fori_loop(0, 5, second_layer, 0)
    finish(10, d0)

    upper = lax.broadcasted_iota(jnp.int32, (8, N), 0) < 4
    for b in range(3):
        blocks = []
        for ref in (rs, re):
            rows = []
            for k in range(N // 8):
                x, y, zz = (ref[2 * k + i, 8 * b : 8 * b + 8, :] for i in range(3))
                y = pltpu.roll(y, 4, 0)
                rows.append(jnp.where(upper, x, y) + jnp.where(upper, y, zz))
            blocks.append(jnp.concatenate(rows, axis=0).T)
        for t in range(TILES):
            for half in range(2):
                block, at = (blocks[0], 16 * t) if t < 8 else (blocks[1], 0)
                at = at + 8 * half
                nat[b, pl.ds(8 + t + 72 * half, 8, stride=9), :] = block[at : at + 8]
        nat[b, 0:8, :] = nat[b, EXT : EXT + 8, :]
    total = nat[0, 7 : 7 + N, :] + nat[1, 8 : 8 + N, :] + nat[2, 9 : 9 + N, :]
    visc_out[...] = jnp.exp(total.T)
    for copy in stores:
        copy.wait()


PACK, CONT, MOM, OWN, SPREAD, QC, QM = 32, 32, 16, 32, 32, 48, 24


def step(state):
    vmem = pl.BlockSpec(memory_space=pltpu.VMEM)
    hbm = pl.BlockSpec(memory_space=HBM)
    whole = jax.ShapeDtypeStruct((LAYERS, N, N), F32)
    return pl.pallas_call(
        step_kernel,
        out_shape=(whole, whole, whole, jax.ShapeDtypeStruct((N, N), F32)),
        in_specs=[vmem] * 15,
        out_specs=[hbm] * 3 + [vmem],
        scratch_shapes=[
            pltpu.VMEM((2, FIELDS, EDGE, N), F32),
            pltpu.VMEM((2, LAYERS, EDGE, N), F32),
            pltpu.VMEM((2, LAYERS, EDGE, N), F32),
            pltpu.VMEM((2, LAYERS, EDGE, N), F32),
            pltpu.VMEM((2, LAYERS, EDGE, N), F32),
            pltpu.VMEM((2, 4, EDGE, N), F32),
            pltpu.VMEM((7, PAD, N), F32),
            pltpu.VMEM((PAD, N), F32),
            pltpu.VMEM((PAD, N), F32),
            pltpu.VMEM((PAD, N), F32),
            pltpu.VMEM((PAD, N), F32),
            pltpu.VMEM((4, TALL, N), F32),
            pltpu.VMEM((4, TALL, N), F32),
            pltpu.VMEM((9, EXT + 16, N), F32),
            pltpu.VMEM((LAYERS, N, N), F32),
            pltpu.VMEM((LAYERS, N, N), F32),
            pltpu.VMEM((LAYERS, N, N), F32),
            pltpu.VMEM((PAIRS // 2, 2, EXT + 32, N), BF16),
            pltpu.VMEM((BLOCK, 2 * N), F32),
            pltpu.VMEM((BLOCK, 2 * N), F32),
            pltpu.VMEM((GROUPS, 24, N), F32),
            pltpu.VMEM((GROUPS, 24, N), F32),
            pltpu.VMEM((3, EXT + 16, N), F32),
            pltpu.SemaphoreType.DMA((3,)),
        ],
        compiler_params=pltpu.CompilerParams(vmem_limit_bytes=24 * 2**20),
        name="step",
    )(*state)


def local(z, v, h, ls, vi, w, grav, conv1, bias1, conv2, bias2, conv3):
    conv1 = jnp.transpose(conv1, (0, 1, 3, 2))
    conv3 = jnp.transpose(conv3, (0, 2, 1, 3))
    held = [pltpu.with_memory_space_constraint(x, HBM) for x in (z, v, h, ls, vi, w, grav, conv1, conv2, conv3, bias1, bias2)]
    return step(exchange(held[:6], *held[6:]))


def solution(mesh):
    block, flat = P(None, "ox", "oy"), P("ox", "oy")
    return jax.shard_map(
        local,
        mesh=mesh,
        in_specs=(block, block, block, flat, flat, block) + (P(),) * 6,
        out_specs=(block, block, block, flat),
        check_vma=False,
    )
```

time: 32.6 us -> 28.5 us (0.87)
  the two profiles are of different devices: /device:TPU:25 before, /device:TPU:0 now
where the time goes in v4:
time: 28.5 us; the launch traced here: 28.4 us
  Pallas kernels  27.7 us (97%)
  between operations  0.64 us (2%)
    pallas_call x1, Pallas kernels, exchange(): pl.pallas_call(exchange_kernel, out_shape=(array(FIELDS, PAD, N), array(L...  15.4 us
    pallas_call x1, Pallas kernels, step(): pl.pallas_call(step_kernel, out_shape=(whole, whole, whole, jax.ShapeDtyp...  12.3 us

profile of v4, /device:TPU:0, one launch (start us, length us, event | category | flops | bytes accessed | tf_op | source)
XLA Modules:
  0.0 28.4 jit_solution(16317297060437207154)
XLA Ops:
  0.6 15.4 %exchange.1 = (f32[16,160,128]{2,1,0:T(8,128)S(1)}, f32[4,160,128]{2,1,0:T(8,128)S(1)}, f32[4,160,128]{2,1,0:T(8,128)S(1)}, f32[4,160,128]{2,1,0:T(8,128)S(1)}, ...) custom-call(f32[4,128,128]{2,1,0:T(8,128)} %z.1, ...), custom_call_target="tpu_custom_call" | custom-call | tf_op jit(solution)/shard_map/exchange/pallas_call | solution.py:261
  16.0 12.3 %step.1 = (f32[4,128,128]{2,1,0:T(8,128)}, f32[4,128,128]{2,1,0:T(8,128)}, f32[4,128,128]{2,1,0:T(8,128)}, f32[128,128]{1,0:T(8,128)}) custom-call(f32[16,160,128]{2,1,0:T(8,128)S(1)} %get-tuple-element.19.f0, f32[4,160,128]{2,1,0:T(8,128)S(1)} %get-tuple-element.20.p0, f32[4,160,128]{2,1,0:T(8,128)S(1)} %get-tuple-element.21.t0, ...), custom_call_target="tpu_custom_call" | custom-call | tf_op jit(solution)/shard_map/step/pallas_call | solution.py:627

commit v5 on v4

--- a/solution.py
+++ b/solution.py
@@ -136,12 +136,20 @@
     east, west = lax.rem(ox + 1, nx), lax.rem(ox + nx - 1, nx)
     above, below = lax.rem(oy + 1, ny), lax.rem(oy + ny - 1, ny)
     peers = (
-        (east, oy), (west, oy), (ox, above), (ox, below),
-        (east, above), (east, below), (west, above), (west, below),
+        (east, oy), (west, oy),
+        (ox, above), (east, above), (west, above),
+        (ox, below), (east, below), (west, below),
     )
     barrier = pltpu.get_barrier_semaphore()
-    for peer in peers:
-        pl.semaphore_signal(barrier, inc=1, device_id=peer, device_id_type=MESH)
+    has_north, has_south = oy < ny - 1, oy > 0
+
+    def greet(first_peer, last_peer):
+        for peer in peers[first_peer:last_peer]:
+            pl.semaphore_signal(barrier, inc=1, device_id=peer, device_id_type=MESH)
+
+    greet(0, 2)
+    pl.when(has_north)(lambda: greet(2, 5))
+    pl.when(has_south)(lambda: greet(5, 8))
     mid = pl.ds(16, N)
     loads = [
         pltpu.make_async_copy(src, dst, load_sem.at[k])
@@ -187,28 +195,47 @@
         return carry
 
     lax.fori_loop(0, N // PACK, pack, 0)
-    pl.semaphore_wait(barrier, 8)
+    pl.semaphore_wait(barrier, 2 + 3 * has_north.astype(jnp.int32) + 3 * has_south.astype(jnp.int32))
 
     first, last = pl.ds(0, 8), pl.ds(N - 8, 8)
-    moves = (
-        (nb, ns.at[1, 8 : 8 + N], (ox, above)),
-        (sb, ns.at[0, 8 : 8 + N], (ox, below)),
-        (f0.at[:, N + 8 : N + 16], xw, (east, oy)),
-        (f0.at[:, 16:24], xe, (west, oy)),
-        (nb.at[last], ns.at[1, 0:8], (east, above)),
-        (sb.at[last], ns.at[0, 0:8], (east, below)),
-        (nb.at[first], ns.at[1, N + 8 : EXT], (west, above)),
-        (sb.at[first], ns.at[0, N + 8 : EXT], (west, below)),
-    )
-    sends = [
-        pltpu.make_async_remote_copy(
+    def move(k, src, dst, peer):
+        return pltpu.make_async_remote_copy(
             src_ref=src, dst_ref=dst, send_sem=send_sem.at[k], recv_sem=recv_sem.at[k],
             device_id=peer, device_id_type=MESH,
         )
-        for k, (src, dst, peer) in enumerate(moves)
-    ]
-    for copy in reversed(sends):
-        copy.start()
+
+    along = (
+        move(0, f0.at[:, N + 8 : N + 16], xw, (east, oy)),
+        move(1, f0.at[:, 16:24], xe, (west, oy)),
+    )
+    northward = (
+        move(2, nb.at[last], ns.at[1, 0:8], (east, above)),
+        move(3, nb.at[first], ns.at[1, N + 8 : EXT], (west, above)),
+        move(4, nb, ns.at[1, 8 : 8 + N], (ox, above)),
+    )
+    southward = (
+        move(5, sb.at[last], ns.at[0, 0:8], (east, below)),
+        move(6, sb.at[first], ns.at[0, N + 8 : EXT], (west, below)),
+        move(7, sb, ns.at[0, 8 : 8 + N], (ox, below)),
+    )
+
+    def start(copies):
+        for copy in copies:
+            copy.start()
+
+    pl.when(has_north)(lambda: start(northward[:2]))
+    pl.when(has_south)(lambda: start(southward[:2]))
+    start(along)
+    pl.when(has_north)(lambda: start(northward[2:]))
+    pl.when(has_south)(lambda: start(southward[2:]))
+
+    @pl.when(jnp.logical_not(has_north))
+    def _():
+        ns[0] = jnp.ones((EXT, N), F32)
+
+    @pl.when(jnp.logical_not(has_south))
+    def _():
+        ns[1] = jnp.ones((EXT, N), F32)
 
     for copy in loads[6:]:
         copy.wait()
@@ -247,8 +274,21 @@
         return carry
 
     lax.fori_loop(0, 6, inner_turn, 0)
-    for copy in sends:
-        copy.wait()
+
+    def sent(copies):
+        for copy in copies:
+            copy.wait_send()
+
+    def received(copies):
+        for copy in copies:
+            copy.wait_recv()
+
+    sent(along)
+    pl.when(has_north)(lambda: sent(northward))
+    pl.when(has_south)(lambda: sent(southward))
+    received(along)
+    pl.when(has_north)(lambda: received(southward))
+    pl.when(has_south)(lambda: received(northward))
 
 
 def exchange(fields, grav, conv1, conv2, conv3, bias1, bias2):
@@ -548,7 +588,8 @@
         ))
         return carry
 
-    lax.fori_loop(0, 7, first_body, 0)
+    for k in range(7):
+        first_body(k, 0)
     for e, (at, inner) in enumerate(((0, 16), (N - 8, 8))):
         merge(8, pl.ds(at, 8), pl.ds(at + 16, 8), (
             (zq, zm, lambda l: ze[e, l, inner : inner + 8, :]),
@@ -583,17 +624,12 @@
             rs[k * STEP + i] = sums[0:24, 0:N]
             re[k * STEP + i, :, 0:16] = sums[0:24, N:EXT]
 
-    second_matmul(0, d0)
-
-    def second_layer(k, carry):
-        second_matmul(2 * k + 1, d1)
-        finish(2 * k, d0)
-        second_matmul(2 * k + 2, d0)
-        finish(2 * k + 1, d1)
-        return carry
-
-    lax.fori_loop(0, 5, second_layer, 0)
-    finish(10, d0)
+    held = (d0, d1)
+    for k in range(11):
+        second_matmul(k, held[k % 2])
+        if k:
+            finish(k - 1, held[(k - 1) % 2])
+    finish(10, held[10 % 2])
 
     upper = lax.broadcasted_iota(jnp.int32, (8, N), 0) < 4
     for b in range(3):
@@ -617,7 +653,7 @@
         copy.wait()
 
 
-PACK, CONT, MOM, OWN, SPREAD, QC, QM = 32, 32, 16, 32, 32, 48, 24
+PACK, CONT, MOM, OWN, SPREAD, QC, QM = 64, 32, 16, 32, 128, 144, 144
 
 
 def step(state):
@@ -650,8 +686,8 @@
             pltpu.VMEM((PAIRS // 2, 2, EXT + 32, N), BF16),
             pltpu.VMEM((BLOCK, 2 * N), F32),
             pltpu.VMEM((BLOCK, 2 * N), F32),
-            pltpu.VMEM((GROUPS, 24, N), F32),
-            pltpu.VMEM((GROUPS, 24, N), F32),
+            pltpu.VMEM((33, 24, N), F32),
+            pltpu.VMEM((33, 24, N), F32),
             pltpu.VMEM((3, EXT + 16, N), F32),
             pltpu.SemaphoreType.DMA((3,)),
         ],

time: 28.5 us -> 23.9 us (0.84)
  the two profiles are of different devices: /device:TPU:0 before, /device:TPU:25 now
where the time goes in v5:
time: 23.9 us; the launch traced here: 23.6 us
  Pallas kernels  23 us (96%)
  between operations  0.64 us (3%)
    pallas_call x1, Pallas kernels, exchange(): pl.pallas_call(exchange_kernel, out_shape=(array(FIELDS, PAD, N), array(L...  13.5 us
    pallas_call x1, Pallas kernels, step(): pl.pallas_call(step_kernel, out_shape=(whole, whole, whole, jax.ShapeDtyp...  9.49 us

profile of v5, /device:TPU:25, one launch (start us, length us, event | category | flops | bytes accessed | tf_op | source)
XLA Modules:
  0.0 23.6 jit_solution(9066598416405083908)
XLA Ops:
  0.6 13.5 %exchange.1 = (f32[16,160,128]{2,1,0:T(8,128)S(1)}, f32[4,160,128]{2,1,0:T(8,128)S(1)}, f32[4,160,128]{2,1,0:T(8,128)S(1)}, f32[4,160,128]{2,1,0:T(8,128)S(1)}, ...) custom-call(f32[4,128,128]{2,1,0:T(8,128)} %z.1, ...), custom_call_target="tpu_custom_call" | custom-call | tf_op jit(solution)/shard_map/exchange/pallas_call | solution.py:301
  14.1 9.5 %step.1 = (f32[4,128,128]{2,1,0:T(8,128)}, f32[4,128,128]{2,1,0:T(8,128)}, f32[4,128,128]{2,1,0:T(8,128)}, f32[128,128]{1,0:T(8,128)}) custom-call(f32[16,160,128]{2,1,0:T(8,128)S(1)} %get-tuple-element.19.f0, f32[4,160,128]{2,1,0:T(8,128)S(1)} %get-tuple-element.20.p0, f32[4,160,128]{2,1,0:T(8,128)S(1)} %get-tuple-element.21.t0, ...), custom_call_target="tpu_custom_call" | custom-call | tf_op jit(solution)/shard_map/step/pallas_call | solution.py:663

commit v6 on v5

--- a/solution.py
+++ b/solution.py
@@ -150,30 +150,35 @@
     greet(0, 2)
     pl.when(has_north)(lambda: greet(2, 5))
     pl.when(has_south)(lambda: greet(5, 8))
-    mid = pl.ds(16, N)
-    loads = [
-        pltpu.make_async_copy(src, dst, load_sem.at[k])
+
+    def load(at, size, sems):
+        here, there = pl.ds(at, size), pl.ds(at + 16, size)
+        pairs = (
+            (ls.at[here], sea_i.at[here]),
+            (z.at[:, here], f0.at[0:4, there]),
+            (v.at[:, here], f0.at[4:8, there]),
+            (h.at[:, here], f0.at[8:12, there]),
+            (vi.at[here], f0.at[VISC, there]),
+            (w.at[:, here], f0.at[WIND : WIND + 2, there]),
+        )
+        return [
+            pltpu.make_async_copy(src, dst, load_sem.at[sems + k]) for k, (src, dst) in enumerate(pairs)
+        ]
+
+    ends = load(0, 8, 0) + load(N - 8, 8, 6)
+    middle = load(8, N - 16, 12)
+    rest = [
+        pltpu.make_async_copy(src, dst, load_sem.at[18 + k])
         for k, (src, dst) in enumerate((
-            (ls, sea_i), (z, f0.at[0:4, mid]), (v, f0.at[4:8, mid]), (h, f0.at[8:12, mid]),
-            (vi, f0.at[VISC, mid]), (w, f0.at[WIND : WIND + 2, mid]),
             (conv1, c1), (conv2, c2), (conv3, c3), (grav_in, grav), (bias1, s1), (bias2, s2),
         ))
     ]
-    for copy in loads:
+    for copy in ends + middle + rest:
         copy.start()
-    ones = jnp.ones((8, N), F32)
-    for rows in (pl.ds(8, 8), pl.ds(N + 16, 8)):
-        for k in range(FIELDS):
-            f0[k, rows, :] = ones
-        for k in range(LAYERS):
-            p0[k, rows, :] = ones
-    for copy in loads[:6]:
-        copy.wait()
-
-    def pack(k, carry):
-        src = pl.ds(pl.multiple_of(PACK * k + 16, 8), PACK)
-        rows = pl.ds(pl.multiple_of(PACK * k, 8), PACK)
-        lane = lanes(PACK)
+
+    def pack(at, size):
+        rows, src = pl.ds(at, size), pl.ds(at + 16, size)
+        lane = lanes(size)
         sea = sea_i[rows, :].astype(F32)
         f0[SEA, src, :] = sea
         to_south = to_north = None
@@ -183,18 +188,23 @@
                 if a < 2:
                     field = field * sea
                     f0[4 * a + l, src, :] = field
-                at = 32 * l + 8 * a
-                moved = pltpu.roll(field, at, 1) if at else field
+                at_lane = 32 * l + 8 * a
+                moved = pltpu.roll(field, at_lane, 1) if at_lane else field
                 if to_south is None:
                     to_south = to_north = moved
                 else:
-                    to_south = jnp.where((lane >= at) & (lane < at + 8), moved, to_south)
-                    to_north = jnp.where((lane >= at - 8) & (lane < at), moved, to_north)
+                    to_south = jnp.where((lane >= at_lane) & (lane < at_lane + 8), moved, to_south)
+                    to_north = jnp.where((lane >= at_lane - 8) & (lane < at_lane), moved, to_north)
         sb[rows, :] = to_south
         nb[rows, :] = to_north
-        return carry
-
-    lax.fori_loop(0, N // PACK, pack, 0)
+
+    for copy in ends:
+        copy.wait()
+    pack(0, 8)
+    pack(N - 8, 8)
+    for copy in middle:
+        copy.wait()
+    pack(8, N - 16)
     pl.semaphore_wait(barrier, 2 + 3 * has_north.astype(jnp.int32) + 3 * has_south.astype(jnp.int32))
 
     first, last = pl.ds(0, 8), pl.ds(N - 8, 8)
@@ -225,9 +235,9 @@
 
     pl.when(has_north)(lambda: start(northward[:2]))
     pl.when(has_south)(lambda: start(southward[:2]))
-    start(along)
     pl.when(has_north)(lambda: start(northward[2:]))
     pl.when(has_south)(lambda: start(southward[2:]))
+    start(along)
 
     @pl.when(jnp.logical_not(has_north))
     def _():
@@ -237,7 +247,13 @@
     def _():
         ns[1] = jnp.ones((EXT, N), F32)
 
-    for copy in loads[6:]:
+    ones = jnp.ones((8, N), F32)
+    for rows in (pl.ds(8, 8), pl.ds(N + 16, 8)):
+        for k in range(FIELDS):
+            f0[k, rows, :] = ones
+        for k in range(LAYERS):
+            p0[k, rows, :] = ones
+    for copy in rest:
         copy.wait()
     build_weights(c1, c2, c3, first_w, second_w, last_w, rows24)
     for l in range(LAYERS):
@@ -321,7 +337,7 @@
             pltpu.SMEM((LAYERS,), F32),
             pltpu.VMEM((HID,), F32),
             pltpu.VMEM((HID,), F32),
-            pltpu.SemaphoreType.DMA((12,)),
+            pltpu.SemaphoreType.DMA((24,)),
             pltpu.SemaphoreType.DMA((8,)),
             pltpu.SemaphoreType.DMA((8,)),
         ],
@@ -653,7 +669,7 @@
         copy.wait()
 
 
-PACK, CONT, MOM, OWN, SPREAD, QC, QM = 64, 32, 16, 32, 128, 144, 144
+CONT, MOM, OWN, SPREAD, QC, QM = 32, 16, 32, 128, 144, 144
 
 
 def step(state):

time: 23.9 us -> 22.4 us (0.937)
  Pallas kernels: 23 us -> 21.7 us
    pallas_call x1, Pallas kernels: 13.5 us -> 12.2 us  [exchange(): pl.pallas_call(exchange_kernel, out_shape=(array(FIELDS, PAD, N), array(L...]
where the time goes in v6:
time: 22.4 us; the launch traced here: 22.3 us
  Pallas kernels  21.7 us (97%)
  between operations  0.64 us (3%)
    pallas_call x1, Pallas kernels, exchange(): pl.pallas_call(exchange_kernel, out_shape=(array(FIELDS, PAD, N), array(L...  12.2 us
    pallas_call x1, Pallas kernels, step(): pl.pallas_call(step_kernel, out_shape=(whole, whole, whole, jax.ShapeDtyp...  9.49 us

profile of v6, /device:TPU:25, one launch (start us, length us, event | category | flops | bytes accessed | tf_op | source)
XLA Modules:
  0.0 22.3 jit_solution(9106542362707222874)
XLA Ops:
  0.6 12.2 %exchange.1 = (f32[16,160,128]{2,1,0:T(8,128)S(1)}, f32[4,160,128]{2,1,0:T(8,128)S(1)}, f32[4,160,128]{2,1,0:T(8,128)S(1)}, f32[4,160,128]{2,1,0:T(8,128)S(1)}, ...) custom-call(f32[4,128,128]{2,1,0:T(8,128)} %z.1, ...), custom_call_target="tpu_custom_call" | custom-call | tf_op jit(solution)/shard_map/exchange/pallas_call | solution.py:317
  12.8 9.5 %step.1 = (f32[4,128,128]{2,1,0:T(8,128)}, f32[4,128,128]{2,1,0:T(8,128)}, f32[4,128,128]{2,1,0:T(8,128)}, f32[128,128]{1,0:T(8,128)}) custom-call(f32[16,160,128]{2,1,0:T(8,128)S(1)} %get-tuple-element.19.f0, f32[4,160,128]{2,1,0:T(8,128)S(1)} %get-tuple-element.20.p0, f32[4,160,128]{2,1,0:T(8,128)S(1)} %get-tuple-element.21.t0, ...), custom_call_target="tpu_custom_call" | custom-call | tf_op jit(solution)/shard_map/step/pallas_call | solution.py:679

commit v7 on v6

--- a/solution.py
+++ b/solution.py
@@ -285,11 +285,11 @@
     lax.fori_loop(0, N // OWN, inner_pack, 0)
 
     def inner_turn(k, carry):
-        rows = pl.ds(pl.multiple_of(16 * k + 24, 8), 32)
-        ft[k] = fs[:, rows, :].reshape(N, N).T
+        block = fs[:, pl.ds(pl.multiple_of(8 * k + 24, 8), 16), :].reshape(HID, N)
+        ft[k] = jnp.concatenate([block, block], axis=0).T
         return carry
 
-    lax.fori_loop(0, 6, inner_turn, 0)
+    lax.fori_loop(0, 13, inner_turn, 0)
 
     def sent(copies):
         for copy in copies:
@@ -319,9 +319,9 @@
         out_shape=(
             array(FIELDS, PAD, N), array(LAYERS, PAD, N), array(LAYERS, PAD, N),
             array(LAYERS, PAD, N), array(LAYERS, PAD, N), array(4, PAD, N),
-            array(6, N, N), array(4, N, N), array(2, EXT, N),
+            array(13, N, N), array(4, N, N), array(2, EXT, N),
             array(FIELDS, 8, N), array(FIELDS, 8, N),
-            array(3 * N, 16 * HID, dtype=BF16), array(18 * HID, 4 * HID, dtype=BF16),
+            array(2 * N, 8 * HID, dtype=BF16), array(18 * HID, 4 * HID, dtype=BF16),
             array(32, 2 * N, dtype=BF16), array(8, N),
         ),
         in_specs=[hbm] * 12,
@@ -362,16 +362,17 @@
     for b in range(3):
         for c in range(4):
             vecs = [jnp.broadcast_to(taps[a, b][c : c + 1], (8, N)) for a in range(3)]
-            for jp in range(8):
+            for jp in range(4):
                 parts = []
-                for i in range(4):
+                for i in range(2):
                     gap = row + 8 * i - 2 * jp - jnp.where(right, 1, 0) - 4
                     val = jnp.zeros((8, N), F32)
                     for a in range(3):
                         val = jnp.where(gap == a, vecs[a], val)
                     parts.append(val)
-                start = 128 * b + 32 * c
-                first_w[start : start + 32, N * jp : N * jp + N] = jnp.concatenate(parts, 0).astype(BF16)
+                start = 64 * b + 16 * c
+                first_w[start : start + 16, N * jp : N * jp + N] = jnp.concatenate(parts, 0).astype(BF16)
+    first_w[192:256, :] = jnp.zeros((64, 8 * HID), BF16)
 
     eye = lax.broadcasted_iota(jnp.int32, (HID, HID), 0) == lax.broadcasted_iota(jnp.int32, (HID, HID), 1)
     eye = jnp.where(eye, 0.5, 0.0).astype(BF16)
@@ -539,21 +540,21 @@
         fs[c, N + 8 : N + 24, :] = fse[1, c, 8:24, :]
 
     row = lax.broadcasted_iota(jnp.int32, (8, N), 0)
-    for k in range(9):
-        if 1 <= k <= 6:
-            inner = ft0[k - 1]
-        else:
-            inner = fs[:, 16 * k + 8 : 16 * k + 40, :].reshape(N, N).T
-        ends = fsq[:, 16 * k + 8 : 16 * k + 40, :].reshape(N, N).T
+    own_tap = lax.broadcasted_iota(jnp.int32, (EXT + 16, N), 1) < HID
+
+    def turned(ref, k):
+        block = ref[:, 8 * k + 8 : 8 * k + 24, :].reshape(HID, N)
+        return jnp.concatenate([block, block], axis=0).T
+
+    for k in range(17):
+        inner = ft0[k - 2] if 2 <= k <= 14 else turned(fs, k)
+        ends = turned(fsq, k)
         low = jnp.where(row < 4, ends[8:16], inner[0:8])
         high = jnp.where(row >= 4, ends[16:24], inner[N - 8 : N])
-        ft[k, 0:8, :] = ends[0:8]
-        ft[k, 8:16, :] = low
-        ft[k, 16:N, :] = inner[8 : N - 8]
-        ft[k, N : N + 8, :] = high
-        ft[k, N + 8 : N + 16, :] = ends[24:32]
-        ft[k, N + 16 : N + 24, :] = ends[0:8]
-        ft[k, N + 24 : N + 32, :] = low
+        whole = jnp.concatenate(
+            [ends[0:8], low, inner[8 : N - 8], high, ends[24:32], ends[0:8], low], axis=0
+        )
+        ft[k] = jnp.where(own_tap, whole, pltpu.roll(whole, EXT + 15, 0))
 
     def merge(size, rows, packed_rows, sources):
         lane = lanes(size)
@@ -576,7 +577,7 @@
 
     def first_layer(k, quarters):
         parts = []
-        for b in range(3):
+        for b in (0, 2):
             pieces = []
             for t in range(TILES):
                 for half in range(2):
@@ -586,7 +587,7 @@
         for quarter in range(quarters):
             out = jnp.dot(left, first_w[:, 256 * quarter : 256 * quarter + 256], preferred_element_type=F32)
             out = activate(out, b1)
-            at = 4 * k + quarter
+            at = 2 * k + quarter
             for p in range(2):
                 one = out[:, N * p : N * p + N]
                 h1[at, p, 16 : 16 + EXT, :] = one.astype(BF16)
@@ -594,7 +595,8 @@
                 h1[at, p, 16 + EXT : 32 + EXT, :] = pltpu.roll(one[0:16], 15, 0).astype(BF16)
 
     def first_body(k, carry):
-        first_layer(k, 4)
+        first_layer(2 * k, 2)
+        first_layer(2 * k + 1, 2)
         rows = pl.ds(pl.multiple_of(16 * k + 8, 8), 16)
         wide = pl.ds(pl.multiple_of(16 * k + 24, 8), 16)
         merge(16, rows, wide, (
@@ -612,8 +614,8 @@
             (vq, vm, lambda l: ve[e, l, inner : inner + 8, :]),
             (hq, hm, lambda l: te[e, l, inner : inner + 8, :]),
         ))
-    first_layer(7, 4)
-    first_layer(8, 2)
+    for k in (14, 15, 16):
+        first_layer(k, 2)
     stores = [
         pltpu.make_async_copy(src, dst, store_sem.at[k])
         for k, (src, dst) in enumerate(((zm, z_out), (vm, v_out), (hm, h_out)))
@@ -695,7 +697,7 @@
             pltpu.VMEM((PAD, N), F32),
             pltpu.VMEM((4, TALL, N), F32),
             pltpu.VMEM((4, TALL, N), F32),
-            pltpu.VMEM((9, EXT + 16, N), F32),
+            pltpu.VMEM((17, EXT + 16, N), F32),
             pltpu.VMEM((LAYERS, N, N), F32),
             pltpu.VMEM((LAYERS, N, N), F32),
             pltpu.VMEM((LAYERS, N, N), F32),

time: 22.4 us -> 22.1 us (0.987)
  Pallas kernels: 21.7 us -> 21.4 us
    pallas_call x1, Pallas kernels: 9.49 us -> 9.19 us  [step(): pl.pallas_call(step_kernel, out_shape=(whole, whole, whole, jax.ShapeDtyp...]
where the time goes in v7:
time: 22.1 us; the launch traced here: 22 us
  Pallas kernels  21.4 us (97%)
  between operations  0.64 us (3%)
    pallas_call x1, Pallas kernels, exchange(): pl.pallas_call(exchange_kernel, out_shape=(array(FIELDS, PAD, N), array(L...  12.2 us
    pallas_call x1, Pallas kernels, step(): pl.pallas_call(step_kernel, out_shape=(whole, whole, whole, jax.ShapeDtyp...  9.19 us

profile of v7, /device:TPU:25, one launch (start us, length us, event | category | flops | bytes accessed | tf_op | source)
XLA Modules:
  0.0 22.0 jit_solution(4863229639662461016)
XLA Ops:
  0.6 12.2 %exchange.1 = (f32[16,160,128]{2,1,0:T(8,128)S(1)}, f32[4,160,128]{2,1,0:T(8,128)S(1)}, f32[4,160,128]{2,1,0:T(8,128)S(1)}, f32[4,160,128]{2,1,0:T(8,128)S(1)}, ...) custom-call(f32[4,128,128]{2,1,0:T(8,128)} %z.1, ...), custom_call_target="tpu_custom_call" | custom-call | tf_op jit(solution)/shard_map/exchange/pallas_call | solution.py:317
  12.8 9.2 %step.1 = (f32[4,128,128]{2,1,0:T(8,128)}, f32[4,128,128]{2,1,0:T(8,128)}, f32[4,128,128]{2,1,0:T(8,128)}, f32[128,128]{1,0:T(8,128)}) custom-call(f32[16,160,128]{2,1,0:T(8,128)S(1)} %get-tuple-element.19.f0, f32[4,160,128]{2,1,0:T(8,128)S(1)} %get-tuple-element.20.p0, f32[4,160,128]{2,1,0:T(8,128)S(1)} %get-tuple-element.21.t0, ...), custom_call_target="tpu_custom_call" | custom-call | tf_op jit(solution)/shard_map/step/pallas_call | solution.py:681

commit v8 on v7

--- a/solution.py
+++ b/solution.py
@@ -554,7 +554,7 @@
         whole = jnp.concatenate(
             [ends[0:8], low, inner[8 : N - 8], high, ends[24:32], ends[0:8], low], axis=0
         )
-        ft[k] = jnp.where(own_tap, whole, pltpu.roll(whole, EXT + 15, 0))
+        ft[k, 0 : EXT + 16, :] = jnp.where(own_tap, whole, pltpu.roll(whole, EXT + 15, 0))
 
     def merge(size, rows, packed_rows, sources):
         lane = lanes(size)
@@ -697,7 +697,7 @@
             pltpu.VMEM((PAD, N), F32),
             pltpu.VMEM((4, TALL, N), F32),
             pltpu.VMEM((4, TALL, N), F32),
-            pltpu.VMEM((17, EXT + 16, N), F32),
+            pltpu.VMEM((17, EXT + 32, N), F32),
             pltpu.VMEM((LAYERS, N, N), F32),
             pltpu.VMEM((LAYERS, N, N), F32),
             pltpu.VMEM((LAYERS, N, N), F32),
@@ -706,7 +706,7 @@
             pltpu.VMEM((BLOCK, 2 * N), F32),
             pltpu.VMEM((33, 24, N), F32),
             pltpu.VMEM((33, 24, N), F32),
-            pltpu.VMEM((3, EXT + 16, N), F32),
+            pltpu.VMEM((3, EXT + 32, N), F32),
             pltpu.SemaphoreType.DMA((3,)),
         ],
         compiler_params=pltpu.CompilerParams(vmem_limit_bytes=24 * 2**20),

time: 22.1 us -> 22.1 us (level)
  no operation moved by 1% of the time
where the time goes in v8:
time: 22.1 us; the launch traced here: 22 us
  Pallas kernels  21.3 us (96%)
  between operations  0.64 us (3%)
    pallas_call x1, Pallas kernels, exchange(): pl.pallas_call(exchange_kernel, out_shape=(array(FIELDS, PAD, N), array(L...  12.2 us
    pallas_call x1, Pallas kernels, step(): pl.pallas_call(step_kernel, out_shape=(whole, whole, whole, jax.ShapeDtyp...  9.18 us

profile of v8, /device:TPU:25, one launch (start us, length us, event | category | flops | bytes accessed | tf_op | source)
XLA Modules:
  0.0 22.0 jit_solution(8602709855111912288)
XLA Ops:
  0.6 12.2 %exchange.1 = (f32[16,160,128]{2,1,0:T(8,128)S(1)}, f32[4,160,128]{2,1,0:T(8,128)S(1)}, f32[4,160,128]{2,1,0:T(8,128)S(1)}, f32[4,160,128]{2,1,0:T(8,128)S(1)}, ...) custom-call(f32[4,128,128]{2,1,0:T(8,128)} %z.1, ...), custom_call_target="tpu_custom_call" | custom-call | tf_op jit(solution)/shard_map/exchange/pallas_call | solution.py:317
  12.8 9.2 %step.1 = (f32[4,128,128]{2,1,0:T(8,128)}, f32[4,128,128]{2,1,0:T(8,128)}, f32[4,128,128]{2,1,0:T(8,128)}, f32[128,128]{1,0:T(8,128)}) custom-call(f32[16,160,128]{2,1,0:T(8,128)S(1)} %get-tuple-element.19.f0, f32[4,160,128]{2,1,0:T(8,128)S(1)} %get-tuple-element.20.p0, f32[4,160,128]{2,1,0:T(8,128)S(1)} %get-tuple-element.21.t0, ...), custom_call_target="tpu_custom_call" | custom-call | tf_op jit(solution)/shard_map/step/pallas_call | solution.py:681
